TPU v7x, 32 devices: a whole 2x2x4 slice. The times are simulated.
32 devices in a mesh: rows: 4 (over y, x), cols: 8 (over z, core).
Axes of the slice: x: 2, y: 2, z: 4, core: 2. Of those that a mesh axis runs over, the one named last changes fastest.
Arguments:
- object_field: float32 [2, 1024, 2048], P(None, 'rows', 'cols'), may hold values from -6 to 6
- probe: float32 [2, 256, 256], replicated, may hold values from -6 to 6
- positions: int32 [4, 8, 6, 2], P('rows', 'cols'), may hold values from 0 to 256
- counts: int32 [4, 8], P('rows', 'cols'), may hold values from 2 to 6
- intensity: int32 [4, 8, 6, 256, 256], P('rows', 'cols'), may hold values from 0 to 4000
Outputs:
- updated_field: float32 [2, 1024, 2048], P(None, 'rows', 'cols')
Inputs may be any that keep to these rules, and one draw needn't show every extreme that they name: Only the first counts[a, b] entries of tile (a, b) in positions and intensity are used.
All inputs are finite; a program needn't handle non-finite values.
Results may differ from a plain program's by a relative error of at most 0.00029.
Values sent between devices are 32-bit elements; how exact they have to be, the bound alone decides.
A program may use at most 64 MiB of HBM per device.

v0:
```python
import functools

import jax
import jax.numpy as jnp
import numpy as np
from jax import lax
from jax.experimental import pallas as pl
from jax.experimental.pallas import tpu as pltpu
from jax.sharding import PartitionSpec as P

MARGIN = 128
ITERS = 2
LANES = 128
ROWS = 8


step_rate = 0.02
photon_unit = 0.001


def tables(length):
    half = length // 2
    k = np.arange(half)[:, None]
    n = np.arange(half)[None, :]
    found = []
    for odd in (0, 1):
        angle = ((2 * k + odd) * n % length) * (2.0 * np.pi / length)
        c = np.cos(angle) / np.sqrt(length)
        s = np.sin(angle) / np.sqrt(length)
        full = np.block([[c, s], [-s, c]])
        found += [full, full.T]
    full = np.stack(found).astype(np.float32)
    high = full.astype(jnp.bfloat16)
    low = (full - high.astype(np.float32)).astype(jnp.bfloat16)
    return np.stack([high, low])


def ordering(length):
    half = length // 2
    index = np.arange(half)
    table = np.zeros((length, length), np.float32)
    table[2 * index, index] = 1
    table[2 * index + 1, half + index] = 1
    return np.stack([table, table.T]).astype(jnp.bfloat16)


def dot(left, right):
    return lax.dot_general(left, right, (((1,), (0,)), ((), ())), preferred_element_type=jnp.float32)


def parted(value):
    high = value.astype(jnp.bfloat16)
    return high, (value - high.astype(jnp.float32)).astype(jnp.bfloat16)


def from_left(table, which, value):
    high, low = parted(value)
    return dot(table[0, which], high) + dot(table[1, which], high) + dot(table[0, which], low)


def from_right(table, which, value):
    high, low = parted(value)
    return dot(high, table[0, which]) + dot(high, table[1, which]) + dot(low, table[0, which])


def order_kernel(counts_ref, order_ref, intensity_ref, out_ref):
    @pl.loop(0, counts_ref[0, 0])
    def _(slot):
        given = intensity_ref[slot]

        def placed(value):
            value = value.astype(jnp.float32).astype(jnp.bfloat16)
            return dot(dot(order_ref[1], value).astype(jnp.bfloat16), order_ref[0])

        out_ref[slot] = (placed(given >> 4) * 16.0 + placed(given & 15)) * photon_unit


def moved_up(value, shift):
    rows, columns = value.shape
    groups = value.reshape(rows // ROWS, ROWS, columns)
    turned = pltpu.roll(groups, (ROWS - shift) % ROWS, 1)
    within = lax.broadcasted_iota(jnp.int32, (1, ROWS, columns), 1) < ROWS - shift
    return jnp.where(within, turned[:-1], turned[1:]).reshape(rows - ROWS, columns)


def moved_down(value, shift):
    rows, columns = value.shape
    groups = value.reshape(rows // ROWS, ROWS, columns)
    turned = pltpu.roll(groups, shift % ROWS, 1)
    none = jnp.zeros((1, ROWS, columns), value.dtype)
    within = lax.broadcasted_iota(jnp.int32, (1, ROWS, columns), 1) >= shift
    lower = jnp.concatenate([turned, none], axis=0)
    upper = jnp.concatenate([none, turned], axis=0)
    return jnp.where(within, lower, upper).reshape(rows + ROWS, columns)


def moved_left(value, shift):
    rows, columns = value.shape
    parts = [pltpu.roll(value[:, c : c + LANES], (LANES - shift) % LANES, 1) for c in range(0, columns, LANES)]
    within = lax.broadcasted_iota(jnp.int32, (rows, LANES), 1) < LANES - shift
    return jnp.concatenate([jnp.where(within, a, b) for a, b in zip(parts[:-1], parts[1:])], axis=1)


def moved_right(value, shift):
    rows, columns = value.shape
    parts = [pltpu.roll(value[:, c : c + LANES], shift % LANES, 1) for c in range(0, columns, LANES)]
    within = lax.broadcasted_iota(jnp.int32, (rows, LANES), 1) >= shift
    none = jnp.zeros((rows, LANES), value.dtype)
    return jnp.concatenate([jnp.where(within, a, b) for a, b in zip(parts + [none], [none] + parts)], axis=1)


def slots_kernel(positions_ref, counts_ref, padded_ref, probe_ref, measured_ref, table_ref, grad_ref):
    size = probe_ref.shape[1]
    half = size // 2
    wide = size + LANES
    last = padded_ref.shape[1] - size - ROWS
    grad_ref[...] = jnp.zeros_like(grad_ref)

    @pl.loop(0, counts_ref[0, 0])
    def _(slot):
        row = positions_ref[slot, 0]
        column = positions_ref[slot, 1]
        start = pl.multiple_of(jnp.where(column >= LANES, LANES, 0), LANES)
        shift = column - start
        first = pl.multiple_of(jnp.minimum(row // ROWS * ROWS, last), ROWS)
        drop = row - first
        there = (pl.ds(first, size + ROWS), pl.ds(start, wide))
        patch_r = moved_left(moved_up(padded_ref[(0, *there)], drop), shift)
        patch_i = moved_left(moved_up(padded_ref[(1, *there)], drop), shift)
        probe_r = probe_ref[0]
        probe_i = probe_ref[1]
        exit_r = probe_r * patch_r - probe_i * patch_i
        exit_i = probe_r * patch_i + probe_i * patch_r
        upper = jnp.concatenate([exit_r[:half], exit_i[:half]], axis=0)
        lower = jnp.concatenate([exit_r[half:], exit_i[half:]], axis=0)
        even = from_left(table_ref, 0, upper + lower)
        odd = from_left(table_ref, 2, upper - lower)
        half_r = jnp.concatenate([even[:half], odd[:half]], axis=0)
        half_i = jnp.concatenate([even[half:], odd[half:]], axis=0)
        left = jnp.concatenate([half_r[:, :half], half_i[:, :half]], axis=1)
        right = jnp.concatenate([half_r[:, half:], half_i[:, half:]], axis=1)
        backs = []
        for odd, value in ((0, left + right), (1, left - right)):
            spec = from_right(table_ref, 2 * odd + 1, value)
            spec_r, spec_i = spec[:, :half], spec[:, half:]
            misfit = spec_r * spec_r + spec_i * spec_i - measured_ref[slot, :, odd * half : (odd + 1) * half]
            scaled = jnp.concatenate([misfit * spec_r, misfit * spec_i], axis=1)
            backs.append(from_right(table_ref, 2 * odd, scaled))
        left = backs[0] + backs[1]
        right = backs[0] - backs[1]
        half_r = jnp.concatenate([left[:, :half], right[:, :half]], axis=1)
        half_i = jnp.concatenate([left[:, half:], right[:, half:]], axis=1)
        even = from_left(table_ref, 1, jnp.concatenate([half_r[:half], half_i[:half]], axis=0))
        odd = from_left(table_ref, 3, jnp.concatenate([half_r[half:], half_i[half:]], axis=0))
        upper = even + odd
        lower = even - odd
        back_r = jnp.concatenate([upper[:half], lower[:half]], axis=0)
        back_i = jnp.concatenate([upper[half:], lower[half:]], axis=0)
        term_r = probe_r * back_r + probe_i * back_i
        term_i = probe_r * back_i - probe_i * back_r
        for part, term in ((0, term_r), (1, term_i)):
            grad_ref[(part, *there)] += moved_down(moved_right(term, shift), drop)


def in_order(counts, intensity, order):
    slots, size, _ = intensity.shape
    return pl.pallas_call(
        order_kernel,
        out_shape=jax.ShapeDtypeStruct((slots, size, size), jnp.float32),
        in_specs=[pl.BlockSpec(memory_space=pltpu.SMEM)] + [pl.BlockSpec(memory_space=pltpu.VMEM)] * 2,
        out_specs=pl.BlockSpec(memory_space=pltpu.VMEM),
        cost_estimate=pl.CostEstimate(
            flops=slots * 4 * size**3, bytes_accessed=slots * 8 * size**2, transcendentals=0
        ),
        compiler_params=pltpu.CompilerParams(vmem_limit_bytes=12 * 1024 * 1024),
        name="order",
    )(counts, order, intensity)


def slot_terms(positions, counts, padded, probe, measured, table):
    slots, size, _ = measured.shape
    return pl.pallas_call(
        slots_kernel,
        out_shape=jax.ShapeDtypeStruct(padded.shape, jnp.float32),
        in_specs=[pl.BlockSpec(memory_space=pltpu.SMEM)] * 2 + [pl.BlockSpec(memory_space=pltpu.VMEM)] * 4,
        out_specs=pl.BlockSpec(memory_space=pltpu.VMEM),
        cost_estimate=pl.CostEstimate(
            flops=slots * 48 * size**3, bytes_accessed=slots * 40 * size**2, transcendentals=0
        ),
        compiler_params=pltpu.CompilerParams(vmem_limit_bytes=20 * 1024 * 1024),
        name="slots",
    )(positions, counts, padded, probe, measured, table)


MESH = pl.DeviceIdType.MESH


class Around:
    def __init__(self, send_sems, recv_sems):
        self.send_sems, self.recv_sems = send_sems, recv_sems
        self.here, self.device = {}, {}
        for axis in ("rows", "cols"):
            count = lax.axis_size(axis)
            me = lax.axis_index(axis)
            self.here[axis, -1], self.here[axis, 1] = me > 0, me < count - 1
            self.device[axis, -1] = {axis: lax.rem(me + count - 1, count)}
            self.device[axis, 1] = {axis: lax.rem(me + 1, count)}

    def meet(self):
        barrier = pltpu.get_barrier_semaphore()
        for side, there in self.here.items():

            @pl.when(there)
            def _():
                pl.semaphore_signal(barrier, inc=1, device_id=self.device[side], device_id_type=MESH)

        pl.semaphore_wait(barrier, sum(there.astype(jnp.int32) for there in self.here.values()))

    def copy(self, index, side, source, target):
        return pltpu.make_async_remote_copy(
            src_ref=source,
            dst_ref=target,
            send_sem=self.send_sems.at[index],
            recv_sem=self.recv_sems.at[index],
            device_id=self.device[side],
            device_id_type=MESH,
        )


def both(first, second):
    return jnp.logical_and(first, second)


def no(flag):
    return jnp.logical_not(flag)


def pad_kernel(field_ref, out_ref, send_sems, recv_sems):
    m = MARGIN
    planes, high, wide = field_ref.shape
    around = Around(send_sems, recv_sems)
    here = around.here
    around.meet()
    row_cuts = {-1: (pl.ds(0, m), pl.ds(m + high, m)), 1: (pl.ds(high - m, m), pl.ds(0, m))}
    col_cuts = {-1: (pl.ds(0, m), pl.ds(m + wide, m)), 1: (pl.ds(wide - m, m), pl.ds(0, m))}
    from_cuts = {-1: pl.ds(0, m), 1: pl.ds(m + high, m)}
    col_from = {-1: pl.ds(m, m), 1: pl.ds(wide, m)}
    rows, cols, corners = {}, {}, {}
    index = 0
    for p in range(planes):
        for d in (-1, 1):
            cut, land = row_cuts[d]
            rows[p, d] = around.copy(
                index, ("rows", d), field_ref.at[p, cut, :], out_ref.at[p, land, pl.ds(m, wide)]
            )
            cut, land = col_cuts[d]
            cols[p, d] = around.copy(
                index + 1, ("cols", d), field_ref.at[p, :, cut], out_ref.at[p, pl.ds(m, high), land]
            )
            index += 2
            for v in (-1, 1):
                corners[p, v, d] = around.copy(
                    index, ("cols", d), out_ref.at[p, from_cuts[v], col_from[d]], out_ref.at[p, from_cuts[v], land]
                )
                index += 1
    for p in range(planes):
        for d in (-1, 1):
            pl.when(here["rows", d])(rows[p, d].start)
    for p in range(planes):
        for d in (-1, 1):
            pl.when(here["cols", d])(cols[p, d].start)
    out_ref[:, m : m + high, m : m + wide] = field_ref[...]
    for v in (-1, 1):

        @pl.when(no(here["rows", v]))
        def _():
            out_ref[:, from_cuts[v], m : m + wide] = jnp.zeros((planes, m, wide), jnp.float32)

        for d in (-1, 1):
            land = col_cuts[-d][1]

            @pl.when(no(both(here["rows", v], here["cols", d])))
            def _():
                out_ref[:, from_cuts[v], land] = jnp.zeros((planes, m, m), jnp.float32)

    for d in (-1, 1):
        land = col_cuts[-d][1]

        @pl.when(no(here["cols", d]))
        def _():
            out_ref[:, m : m + high, land] = jnp.zeros((planes, high, m), jnp.float32)

    for p in range(planes):
        for v in (-1, 1):
            pl.when(here["rows", v])(rows[p, -v].wait_recv)
            for d in (-1, 1):
                pl.when(both(here["rows", v], here["cols", d]))(corners[p, v, d].start)
    for p in range(planes):
        for d in (-1, 1):
            pl.when(here["cols", d])(cols[p, -d].wait_recv)
            for v in (-1, 1):
                pl.when(both(here["rows", v], here["cols", d]))(corners[p, v, -d].wait_recv)
    for p in range(planes):
        for d in (-1, 1):
            pl.when(here["rows", d])(rows[p, d].wait_send)
            pl.when(here["cols", d])(cols[p, d].wait_send)
            for v in (-1, 1):
                pl.when(both(here["rows", v], here["cols", d]))(corners[p, v, d].wait_send)


def step_kernel(last, grad_ref, padded_ref, out_ref, mid_ref, side_ref, band_ref, send_sems, recv_sems):
    m = MARGIN
    planes, extent, _ = grad_ref.shape
    tall = extent // 2
    wide = extent - 2 * m
    around = Around(send_sems, recv_sems)
    here = around.here
    around.meet()
    chains = [(p, h) for p in range(planes) for h in (-1, 1)]
    halves = {-1: pl.ds(0, tall), 1: pl.ds(tall, tall)}
    own = {-1: pl.ds(m, tall - m), 1: pl.ds(tall, tall - m)}
    sides, bands, edges = {}, {}, {}
    index = 0
    cut = {-1: pl.ds(0, m), 1: pl.ds(extent - m, m)}
    inner = {-1: pl.ds(m, m), 1: pl.ds(wide, m)}
    for p, h in chains:
        for d in (-1, 1):
            slot = (d + 1) // 2
            sides[p, h, d] = around.copy(
                index, ("cols", d), grad_ref.at[p, halves[h], cut[d]], side_ref.at[slot, p, halves[h]]
            )
            index += 1
            if not last:
                edges[p, h, d] = around.copy(
                    index, ("cols", d), out_ref.at[p, halves[h], inner[d]], out_ref.at[p, halves[h], cut[-d]]
                )
                index += 1
        if last:
            goes, lands = cut[h], own[-h]
        else:
            goes, lands = halves[h], halves[-h]
        bands[p, h] = around.copy(index, ("rows", h), mid_ref.at[p, goes], band_ref.at[p, lands])
        index += 1
    for p, h in chains:
        for d in (-1, 1):
            pl.when(here["cols", d])(sides[p, h, d].start)
    if not last:
        for d in (-1, 1):

            @pl.when(no(here["cols", d]))
            def _():
                out_ref[:, :, cut[d]] = jnp.zeros((planes, extent, m), jnp.float32)

    for p, h in chains:
        mid_ref[p, halves[h]] = grad_ref[p, halves[h], m : m + wide]
        for d in (-1, 1):
            slot = (1 - d) // 2
            target = pl.ds(0, m) if d < 0 else pl.ds(wide - m, m)

            @pl.when(here["cols", d])
            def _():
                sides[p, h, -d].wait_recv()
                mid_ref[p, halves[h], target] += side_ref[slot, p, halves[h]]

        pl.when(here["rows", h])(bands[p, h].start)
    for p, h in chains:
        whole = own[h] if last else halves[h]

        @pl.when(here["rows", h])
        def _():
            bands[p, -h].wait_recv()
            total = mid_ref[p, whole] + band_ref[p, whole]
            value = padded_ref[p, whole, m : m + wide] - step_rate * total
            if last:
                out_ref[p, pl.ds(own[h].start - m, tall - m)] = value
            else:
                out_ref[p, whole, m : m + wide] = value

        @pl.when(no(here["rows", h]))
        def _():
            value = padded_ref[p, own[h], m : m + wide] - step_rate * mid_ref[p, own[h]]
            if last:
                out_ref[p, pl.ds(own[h].start - m, tall - m)] = value
            else:
                out_ref[p, own[h], m : m + wide] = value
                out_ref[p, cut[h], m : m + wide] = jnp.zeros((m, wide), jnp.float32)

        if not last:
            for d in (-1, 1):
                pl.when(here["cols", d])(edges[p, h, d].start)
    for p, h in chains:
        for d in (-1, 1):
            if not last:
                pl.when(here["cols", d])(edges[p, h, -d].wait_recv)
                pl.when(here["cols", d])(edges[p, h, d].wait_send)
            pl.when(here["cols", d])(sides[p, h, d].wait_send)
        pl.when(here["rows", h])(bands[p, h].wait_send)


def exchange(kernel, name, collective_id, shape, scratch, copies, *arrays):
    return pl.pallas_call(
        kernel,
        out_shape=jax.ShapeDtypeStruct(shape, jnp.float32),
        in_specs=[pl.BlockSpec(memory_space=pltpu.VMEM)] * len(arrays),
        out_specs=pl.BlockSpec(memory_space=pltpu.VMEM),
        scratch_shapes=[pltpu.VMEM(s, jnp.float32) for s in scratch]
        + [pltpu.SemaphoreType.DMA((copies,)), pltpu.SemaphoreType.DMA((copies,))],
        compiler_params=pltpu.CompilerParams(
            collective_id=collective_id, has_side_effects=True, vmem_limit_bytes=12 * 1024 * 1024
        ),
        name=name,
    )(*arrays)


def on_device(object_field, probe, positions, counts, intensity):
    planes, high, wide = object_field.shape
    size = probe.shape[1]
    table = jnp.asarray(tables(size))
    order = jnp.asarray(ordering(size))
    positions = positions[0, 0]
    measured = in_order(counts, intensity[0, 0], order)
    tall, broad = high + 2 * MARGIN, wide + 2 * MARGIN
    outer = (planes, tall, broad)
    scratch = [(planes, tall, wide), (2, planes, tall, MARGIN), (planes, tall, wide)]
    padded = exchange(pad_kernel, "pad", 0, outer, [], 8 * planes, object_field)
    for step in range(ITERS):
        grad = slot_terms(positions, counts, padded, probe, measured, table)
        last = step == ITERS - 1
        kernel = functools.partial(step_kernel, last)
        shape = object_field.shape if last else outer
        padded = exchange(kernel, "step", 1 + step, shape, scratch, 10 * planes, grad, padded)
    return padded


def solution(mesh):
    placed = (
        P(None, "rows", "cols"),
        P(),
        P("rows", "cols", None, None),
        P("rows", "cols"),
        P("rows", "cols", None, None, None),
    )
    return jax.shard_map(
        on_device, mesh=mesh, in_specs=placed, out_specs=P(None, "rows", "cols"), check_vma=False
    )
```

profile of v0, /device:TPU:14, one launch (start us, length us, event | category | flops | bytes accessed | tf_op | source)
XLA Modules:
  0.0 100.4 jit_solution(7847577501615902415)
XLA Ops:
  0.7 0.8 copy.9.positions_ref
  1.4 0.0 copy-start
  1.4 1.4 %copy-done = s32[1,1,6,256,256]{4,3,2,1,0:T(8,128)S(1)} copy-done((s32[1,1,6,256,256]{4,3,2,1,0:T(8,128)S(1)}, s32[1,1,6,256,256]{4,3,2,1,0:T(8,128)}, u32[]{:S(2)}) %copy-start) | copy-done | bytes 1572888
  2.8 0.0 copy-start.2
  2.8 0.9 copy-done.2
  3.8 0.0 copy-start.1
  3.8 1.6 %order.1.measured_ref = f32[6,256,256]{2,1,0:T(8,128)S(1)} custom-call(s32[1,1]{1,0:T(1,128)S(6)} %copy.11.counts_ref, bf16[2,256,256]{2,1,0:T(8,128)(2,1)S(1)} %copy-done.2, s32[6,256,256]{2,1,0:T(8,128)S(1)} %bitcast.2), custom_call_target="tpu_custom_call" | custom-call | flops 402653184 | bytes 3145728 | tf_op jit(solution)/shard_map/order/pallas_call | solution.py:167
  5.4 0.0 copy-done.1
  5.4 0.0 copy-start.3
  5.4 0.0 copy-start.4
  5.5 17.0 %pad.1.padded_ref = f32[2,512,512]{2,1,0:T(8,128)S(1)} custom-call(f32[2,256,256]{2,1,0:T(8,128)S(1)} %copy-done.1), custom_call_target="tpu_custom_call" | custom-call | tf_op jit(solution)/shard_map/pad/pallas_call | solution.py:401
  22.4 0.0 copy-done.3
  22.4 0.0 copy-done.4
  22.5 8.7 %slots.2.grad_ref = f32[2,512,512]{2,1,0:T(8,128)S(1)} custom-call(s32[6,2]{1,0:T(8,128)S(1)} %copy.9.positions_ref, s32[1,1]{1,0:T(1,128)S(6)} %copy.11.counts_ref, f32[2,512,512]{2,1,0:T(8,128)S(1)} %pad.1.padded_ref, f32[2,256,256]{2,1,0:T(8,128)S(1)} %copy-done.3, f32[6,256,256]{2,1,0:T(8,128)S(1)} %order.1.measured_ref, ...), custom_call_target="tpu_custom_call" | custom-call | flops 4831838208 | bytes 15728640 | tf_op jit(solution)/shard_map/slots/pallas_call | solution.py:182
  31.2 36.7 %step.2.padded_ref = f32[2,512,512]{2,1,0:T(8,128)S(1)} custom-call(f32[2,512,512]{2,1,0:T(8,128)S(1)} %slots.2.grad_ref, f32[2,512,512]{2,1,0:T(8,128)S(1)} %pad.1.padded_ref), custom_call_target="tpu_custom_call" | custom-call | tf_op jit(solution)/shard_map/step/pallas_call | solution.py:401
  67.9 8.7 %slots.3.grad_ref = f32[2,512,512]{2,1,0:T(8,128)S(1)} custom-call(s32[6,2]{1,0:T(8,128)S(1)} %copy.9.positions_ref, s32[1,1]{1,0:T(1,128)S(6)} %copy.11.counts_ref, f32[2,512,512]{2,1,0:T(8,128)S(1)} %step.2.padded_ref, f32[2,256,256]{2,1,0:T(8,128)S(1)} %copy-done.3, f32[6,256,256]{2,1,0:T(8,128)S(1)} %order.1.measured_ref, ...), custom_call_target="tpu_custom_call" | custom-call | flops 4831838208 | bytes 15728640 | tf_op jit(solution)/shard_map/slots/pallas_call | solution.py:182
  76.7 23.0 %step.3 = f32[2,256,256]{2,1,0:T(8,128)S(1)} custom-call(f32[2,512,512]{2,1,0:T(8,128)S(1)} %slots.3.grad_ref, f32[2,512,512]{2,1,0:T(8,128)S(1)} %step.2.padded_ref), custom_call_target="tpu_custom_call" | custom-call | tf_op jit(solution)/shard_map/step/pallas_call | solution.py:401
  99.6 0.8 copy.12
Async XLA Ops:
  1.4 1.4 %copy-start = (s32[1,1,6,256,256]{4,3,2,1,0:T(8,128)S(1)}, s32[1,1,6,256,256]{4,3,2,1,0:T(8,128)}, u32[]{:S(2)}) copy-start(s32[1,1,6,256,256]{4,3,2,1,0:T(8,128)} %param.11) | copy-start | bytes 4718596
  2.8 0.9 copy-start.2
  3.8 1.6 %copy-start.1 = (f32[2,256,256]{2,1,0:T(8,128)S(1)}, f32[2,256,256]{2,1,0:T(8,128)}, u32[]{:S(2)}) copy-start(f32[2,256,256]{2,1,0:T(8,128)} %field_ref.1) | copy-start | bytes 1572868
  5.4 17.0 %copy-start.3 = (f32[2,256,256]{2,1,0:T(8,128)S(1)}, f32[2,256,256]{2,1,0:T(8,128)}, u32[]{:S(2)}) copy-start(f32[2,256,256]{2,1,0:T(8,128)} %probe_ref.3) | copy-start | bytes 1572868
  5.4 17.0 %copy-start.4 = (bf16[2,4,256,256]{3,2,1,0:T(8,128)(2,1)S(1)}, bf16[2,4,256,256]{3,2,1,0:T(8,128)(2,1)}, u32[]{:S(2)}) copy-start(bf16[2,4,256,256]{3,2,1,0:T(8,128)(2,1)} %constant.4.clone.table_ref) | copy-start | bytes 3145732
where the time goes:
time: 101 us; the launch traced here: 100 us
  Pallas kernels  95.8 us (95%)
  local copies, waits for them, and re-layouts  3.94 us (4%)
    pallas_call x3, Pallas kernels, exchange(): pl.pallas_call(kernel, out_shape=jax.ShapeDtypeStruct(shape, jnp.float32)...  76.7 us
    pallas_call x2, Pallas kernels, slot_terms(): pl.pallas_call(slots_kernel, out_shape=jax.ShapeDtypeStruct(padded.shape,...  17.4 us
    unnamed x11, local copies, waits for them, and re-layouts  3.17 us

commit v1 on v0

--- a/solution.py
+++ b/solution.py
@@ -118,8 +118,8 @@
 
     @pl.loop(0, counts_ref[0, 0])
     def _(slot):
-        row = positions_ref[slot, 0]
-        column = positions_ref[slot, 1]
+        row = positions_ref[0, 0, slot, 0]
+        column = positions_ref[0, 0, slot, 1]
         start = pl.multiple_of(jnp.where(column >= LANES, LANES, 0), LANES)
         shift = column - start
         first = pl.multiple_of(jnp.minimum(row // ROWS * ROWS, last), ROWS)
@@ -198,35 +198,95 @@
 class Around:
     def __init__(self, send_sems, recv_sems):
         self.send_sems, self.recv_sems = send_sems, recv_sems
+        self.sends = self.recvs = 0
         self.here, self.device = {}, {}
         for axis in ("rows", "cols"):
             count = lax.axis_size(axis)
             me = lax.axis_index(axis)
-            self.here[axis, -1], self.here[axis, 1] = me > 0, me < count - 1
-            self.device[axis, -1] = {axis: lax.rem(me + count - 1, count)}
-            self.device[axis, 1] = {axis: lax.rem(me + 1, count)}
+            for d in (-2, -1, 1, 2):
+                self.here[axis, d] = me + d >= 0 if d < 0 else me + d < count
+                self.device[axis, d] = {axis: lax.rem(me + count + d, count)}
+        count = lax.axis_size("rows")
+        self.relays = count > 2 and count % 2 == 0
+        odd = lax.rem(lax.axis_index("rows"), 2) == 1
+        self.far = {1: odd, -1: no(odd)}
 
     def meet(self):
         barrier = pltpu.get_barrier_semaphore()
-        for side, there in self.here.items():
-
-            @pl.when(there)
+        sides = [("rows", -1), ("rows", 1), ("cols", -1), ("cols", 1)]
+        if self.relays:
+            sides += [("rows", -2), ("rows", 2)]
+        for side in sides:
+
+            @pl.when(self.here[side])
             def _():
                 pl.semaphore_signal(barrier, inc=1, device_id=self.device[side], device_id_type=MESH)
 
-        pl.semaphore_wait(barrier, sum(there.astype(jnp.int32) for there in self.here.values()))
-
-    def copy(self, index, side, source, target):
+        pl.semaphore_wait(barrier, sum(self.here[side].astype(jnp.int32) for side in sides))
+
+    def new_recv(self):
+        self.recvs += 1
+        return self.recvs - 1
+
+    def copy(self, side, source, target, recv=None):
+        recv = self.new_recv() if recv is None else recv
+        self.sends += 1
         return pltpu.make_async_remote_copy(
             src_ref=source,
             dst_ref=target,
-            send_sem=self.send_sems.at[index],
-            recv_sem=self.recv_sems.at[index],
+            send_sem=self.send_sems.at[self.sends - 1],
+            recv_sem=self.recv_sems.at[recv],
             device_id=self.device[side],
             device_id_type=MESH,
         )
 
 
+class Side:
+    def __init__(self, around, axis, d, source, target):
+        self.here, self.back = around.here[axis, d], around.here[axis, -d]
+        self.straight = around.copy((axis, d), source, target)
+
+    def start(self):
+        pl.when(self.here)(self.straight.start)
+
+    def wait_recv(self):
+        pl.when(self.back)(self.straight.wait_recv)
+
+    def wait_send(self):
+        pl.when(self.here)(self.straight.wait_send)
+
+
+class Hop:
+    def __init__(self, around, d, source, target, relay):
+        here, far = around.here["rows", d], around.far[d]
+        self.back = around.here["rows", -d]
+        recv = around.new_recv()
+        self.straight = around.copy(("rows", d), source, target, recv)
+        self.near = both(here, no(far))
+        self.long = both(here, far)
+        self.middle = both(around.here["rows", -2 * d], far)
+        self.first = around.copy(("rows", 2 * d), source, relay)
+        self.second = around.copy(("rows", -d), relay, target, recv)
+
+    def start(self):
+        pl.when(self.near)(self.straight.start)
+        pl.when(self.long)(self.first.start)
+
+    def forward(self):
+        @pl.when(self.middle)
+        def _():
+            self.first.wait_recv()
+            self.second.start()
+
+    def wait_recv(self):
+        pl.when(self.back)(self.straight.wait_recv)
+
+    def wait_send(self):
+        pl.when(self.near)(self.straight.wait_send)
+        pl.when(self.long)(self.first.wait_send)
+        pl.when(self.middle)(self.second.wait_send)
+
+
 def both(first, second):
     return jnp.logical_and(first, second)
 
@@ -235,7 +295,7 @@
     return jnp.logical_not(flag)
 
 
-def pad_kernel(field_ref, out_ref, send_sems, recv_sems):
+def pad_kernel(field_ref, out_ref, relay_ref, send_sems, recv_sems):
     m = MARGIN
     planes, high, wide = field_ref.shape
     around = Around(send_sems, recv_sems)
@@ -246,29 +306,26 @@
     from_cuts = {-1: pl.ds(0, m), 1: pl.ds(m + high, m)}
     col_from = {-1: pl.ds(m, m), 1: pl.ds(wide, m)}
     rows, cols, corners = {}, {}, {}
-    index = 0
     for p in range(planes):
         for d in (-1, 1):
             cut, land = row_cuts[d]
-            rows[p, d] = around.copy(
-                index, ("rows", d), field_ref.at[p, cut, :], out_ref.at[p, land, pl.ds(m, wide)]
-            )
+            source, target = field_ref.at[p, cut, :], out_ref.at[p, land, pl.ds(m, wide)]
+            if around.relays and p == 0:
+                rows[p, d] = Hop(around, d, source, target, relay_ref.at[0, 0])
+            else:
+                rows[p, d] = Side(around, "rows", d, source, target)
             cut, land = col_cuts[d]
-            cols[p, d] = around.copy(
-                index + 1, ("cols", d), field_ref.at[p, :, cut], out_ref.at[p, pl.ds(m, high), land]
-            )
-            index += 2
+            cols[p, d] = Side(around, "cols", d, field_ref.at[p, :, cut], out_ref.at[p, pl.ds(m, high), land])
             for v in (-1, 1):
                 corners[p, v, d] = around.copy(
-                    index, ("cols", d), out_ref.at[p, from_cuts[v], col_from[d]], out_ref.at[p, from_cuts[v], land]
+                    ("cols", d), out_ref.at[p, from_cuts[v], col_from[d]], out_ref.at[p, from_cuts[v], land]
                 )
-                index += 1
     for p in range(planes):
         for d in (-1, 1):
-            pl.when(here["rows", d])(rows[p, d].start)
+            rows[p, d].start()
     for p in range(planes):
         for d in (-1, 1):
-            pl.when(here["cols", d])(cols[p, d].start)
+            cols[p, d].start()
     out_ref[:, m : m + high, m : m + wide] = field_ref[...]
     for v in (-1, 1):
 
@@ -290,60 +347,60 @@
         def _():
             out_ref[:, m : m + high, land] = jnp.zeros((planes, high, m), jnp.float32)
 
-    for p in range(planes):
+    if around.relays:
+        for d in (-1, 1):
+            rows[0, d].forward()
+    for p in reversed(range(planes)):
         for v in (-1, 1):
-            pl.when(here["rows", v])(rows[p, -v].wait_recv)
+            rows[p, -v].wait_recv()
             for d in (-1, 1):
                 pl.when(both(here["rows", v], here["cols", d]))(corners[p, v, d].start)
     for p in range(planes):
         for d in (-1, 1):
-            pl.when(here["cols", d])(cols[p, -d].wait_recv)
+            cols[p, -d].wait_recv()
             for v in (-1, 1):
                 pl.when(both(here["rows", v], here["cols", d]))(corners[p, v, -d].wait_recv)
     for p in range(planes):
         for d in (-1, 1):
-            pl.when(here["rows", d])(rows[p, d].wait_send)
-            pl.when(here["cols", d])(cols[p, d].wait_send)
+            rows[p, d].wait_send()
+            cols[p, d].wait_send()
             for v in (-1, 1):
                 pl.when(both(here["rows", v], here["cols", d]))(corners[p, v, d].wait_send)
 
 
-def step_kernel(last, grad_ref, padded_ref, out_ref, mid_ref, side_ref, band_ref, send_sems, recv_sems):
+def step_kernel(last, grad_ref, padded_ref, out_ref, mid_ref, side_ref, band_ref, relay_ref, send_sems, recv_sems):
     m = MARGIN
     planes, extent, _ = grad_ref.shape
-    tall = extent // 2
     wide = extent - 2 * m
+    part = extent // 4
     around = Around(send_sems, recv_sems)
     here = around.here
     around.meet()
-    chains = [(p, h) for p in range(planes) for h in (-1, 1)]
-    halves = {-1: pl.ds(0, tall), 1: pl.ds(tall, tall)}
-    own = {-1: pl.ds(m, tall - m), 1: pl.ds(tall, tall - m)}
-    sides, bands, edges = {}, {}, {}
-    index = 0
+    begin = {(-1, 0): 0, (-1, 1): part, (1, 1): 2 * part, (1, 0): 3 * part}
+    lines = {key: pl.ds(start, part) for key, start in begin.items()}
     cut = {-1: pl.ds(0, m), 1: pl.ds(extent - m, m)}
     inner = {-1: pl.ds(m, m), 1: pl.ds(wide, m)}
-    for p, h in chains:
+    blocks = {q: [(p, h, q) for p in range(planes) for h in (-1, 1)] for q in (0, 1)}
+    sides, bands, edges = {}, {}, {}
+    for p, h, q in blocks[0] + blocks[1]:
         for d in (-1, 1):
             slot = (d + 1) // 2
-            sides[p, h, d] = around.copy(
-                index, ("cols", d), grad_ref.at[p, halves[h], cut[d]], side_ref.at[slot, p, halves[h]]
+            sides[p, h, q, d] = Side(
+                around, "cols", d, grad_ref.at[p, lines[h, q], cut[d]], side_ref.at[slot, p, lines[h, q]]
             )
-            index += 1
             if not last:
-                edges[p, h, d] = around.copy(
-                    index, ("cols", d), out_ref.at[p, halves[h], inner[d]], out_ref.at[p, halves[h], cut[-d]]
+                edges[p, h, q, d] = Side(
+                    around, "cols", d, out_ref.at[p, lines[h, q], inner[d]], out_ref.at[p, lines[h, q], cut[-d]]
                 )
-                index += 1
-        if last:
-            goes, lands = cut[h], own[-h]
+        if last and q == 1:
+            continue
+        source, target = mid_ref.at[p, lines[h, q]], band_ref.at[p, lines[-h, 1 - q]]
+        if around.relays and (p == 0 if last else q == 0):
+            bands[p, h, q] = Hop(around, h, source, target, relay_ref.at[p, 0])
         else:
-            goes, lands = halves[h], halves[-h]
-        bands[p, h] = around.copy(index, ("rows", h), mid_ref.at[p, goes], band_ref.at[p, lands])
-        index += 1
-    for p, h in chains:
-        for d in (-1, 1):
-            pl.when(here["cols", d])(sides[p, h, d].start)
+            bands[p, h, q] = Side(around, "rows", h, source, target)
+    for key in sides:
+        sides[key].start()
     if not last:
         for d in (-1, 1):
 
@@ -351,50 +408,55 @@
             def _():
                 out_ref[:, :, cut[d]] = jnp.zeros((planes, extent, m), jnp.float32)
 
-    for p, h in chains:
-        mid_ref[p, halves[h]] = grad_ref[p, halves[h], m : m + wide]
+    for p, h, q in blocks[0] + blocks[1]:
+        mid_ref[p, lines[h, q]] = grad_ref[p, lines[h, q], m : m + wide]
         for d in (-1, 1):
             slot = (1 - d) // 2
             target = pl.ds(0, m) if d < 0 else pl.ds(wide - m, m)
 
             @pl.when(here["cols", d])
             def _():
-                sides[p, h, -d].wait_recv()
-                mid_ref[p, halves[h], target] += side_ref[slot, p, halves[h]]
-
-        pl.when(here["rows", h])(bands[p, h].start)
-    for p, h in chains:
-        whole = own[h] if last else halves[h]
+                sides[p, h, q, -d].straight.wait_recv()
+                mid_ref[p, lines[h, q], target] += side_ref[slot, p, lines[h, q]]
+
+        if (p, h, q) in bands:
+            bands[p, h, q].start()
+    for band in bands.values():
+        if isinstance(band, Hop):
+            band.forward()
+    for p, h, q in blocks[0] + blocks[1]:
+        rows = lines[h, q]
+        if last and q == 0:
+            continue
 
         @pl.when(here["rows", h])
         def _():
-            bands[p, -h].wait_recv()
-            total = mid_ref[p, whole] + band_ref[p, whole]
-            value = padded_ref[p, whole, m : m + wide] - step_rate * total
+            bands[p, -h, 1 - q].straight.wait_recv()
+            total = mid_ref[p, rows] + band_ref[p, rows]
+            value = padded_ref[p, rows, m : m + wide] - step_rate * total
             if last:
-                out_ref[p, pl.ds(own[h].start - m, tall - m)] = value
+                out_ref[p, pl.ds(rows.start - m, part)] = value
             else:
-                out_ref[p, whole, m : m + wide] = value
+                out_ref[p, rows, m : m + wide] = value
 
         @pl.when(no(here["rows", h]))
         def _():
-            value = padded_ref[p, own[h], m : m + wide] - step_rate * mid_ref[p, own[h]]
-            if last:
-                out_ref[p, pl.ds(own[h].start - m, tall - m)] = value
+            if q == 0:
+                out_ref[p, rows, m : m + wide] = jnp.zeros((part, wide), jnp.float32)
             else:
-                out_ref[p, own[h], m : m + wide] = value
-                out_ref[p, cut[h], m : m + wide] = jnp.zeros((m, wide), jnp.float32)
+                value = padded_ref[p, rows, m : m + wide] - step_rate * mid_ref[p, rows]
+                if last:
+                    out_ref[p, pl.ds(rows.start - m, part)] = value
+                else:
+                    out_ref[p, rows, m : m + wide] = value
 
         if not last:
             for d in (-1, 1):
-                pl.when(here["cols", d])(edges[p, h, d].start)
-    for p, h in chains:
-        for d in (-1, 1):
-            if not last:
-                pl.when(here["cols", d])(edges[p, h, -d].wait_recv)
-                pl.when(here["cols", d])(edges[p, h, d].wait_send)
-            pl.when(here["cols", d])(sides[p, h, d].wait_send)
-        pl.when(here["rows", h])(bands[p, h].wait_send)
+                edges[p, h, q, d].start()
+    for edge in edges.values():
+        edge.wait_recv()
+    for copy in [*edges.values(), *sides.values(), *bands.values()]:
+        copy.wait_send()
 
 
 def exchange(kernel, name, collective_id, shape, scratch, copies, *arrays):
@@ -417,18 +479,18 @@
     size = probe.shape[1]
     table = jnp.asarray(tables(size))
     order = jnp.asarray(ordering(size))
-    positions = positions[0, 0]
     measured = in_order(counts, intensity[0, 0], order)
     tall, broad = high + 2 * MARGIN, wide + 2 * MARGIN
     outer = (planes, tall, broad)
-    scratch = [(planes, tall, wide), (2, planes, tall, MARGIN), (planes, tall, wide)]
-    padded = exchange(pad_kernel, "pad", 0, outer, [], 8 * planes, object_field)
+    relay = (planes, 2, MARGIN, wide)
+    scratch = [(planes, tall, wide), (2, planes, tall, MARGIN), (planes, tall, wide), relay]
+    padded = exchange(pad_kernel, "pad", 0, outer, [relay], 16 * planes, object_field)
     for step in range(ITERS):
         grad = slot_terms(positions, counts, padded, probe, measured, table)
         last = step == ITERS - 1
         kernel = functools.partial(step_kernel, last)
         shape = object_field.shape if last else outer
-        padded = exchange(kernel, "step", 1 + step, shape, scratch, 10 * planes, grad, padded)
+        padded = exchange(kernel, "step", 1 + step, shape, scratch, 32 * planes, grad, padded)
     return padded
 
 

time: 101 us -> 93.9 us (0.930)
  the two profiles are of different devices: /device:TPU:14 before, /device:TPU:5 now
where the time goes in v1:
time: 93.9 us; the launch traced here: 92 us
  Pallas kernels  87.3 us (93%)
  local copies, waits for them, and re-layouts  3.94 us (4%)
    pallas_call x3, Pallas kernels, exchange(): pl.pallas_call(kernel, out_shape=jax.ShapeDtypeStruct(shape, jnp.float32)...  72.7 us
    pallas_call x2, Pallas kernels, slot_terms(): pl.pallas_call(slots_kernel, out_shape=jax.ShapeDtypeStruct(padded.shape,...  13.5 us
    unnamed x12, local copies, waits for them, and re-layouts  3.94 us

profile of v1, /device:TPU:5, one launch (start us, length us, event | category | flops | bytes accessed | tf_op | source)
XLA Modules:
  0.0 92.0 jit_solution(13952127874412777950)
XLA Ops:
  0.7 0.8 copy.9.positions_ref
  1.4 0.0 copy-start
  1.4 1.4 %copy-done = s32[1,1,6,256,256]{4,3,2,1,0:T(8,128)S(1)} copy-done((s32[1,1,6,256,256]{4,3,2,1,0:T(8,128)S(1)}, s32[1,1,6,256,256]{4,3,2,1,0:T(8,128)}, u32[]{:S(2)}) %copy-start) | copy-done | bytes 1572888
  2.8 0.0 copy-start.2
  2.8 0.9 %copy-done.2 = bf16[2,256,256]{2,1,0:T(8,128)(2,1)S(1)} copy-done((bf16[2,256,256]{2,1,0:T(8,128)(2,1)S(1)}, bf16[2,256,256]{2,1,0:T(8,128)(2,1)}, u32[]{:S(2)}) %copy-start.2) | copy-done | bytes 262168
  3.8 0.0 copy-start.1
  3.8 1.2 %order.1.measured_ref = f32[6,256,256]{2,1,0:T(8,128)S(1)} custom-call(s32[1,1]{1,0:T(1,128)S(6)} %copy.11.counts_ref, bf16[2,256,256]{2,1,0:T(8,128)(2,1)S(1)} %copy-done.2, s32[6,256,256]{2,1,0:T(8,128)S(1)} %bitcast.1), custom_call_target="tpu_custom_call" | custom-call | flops 402653184 | bytes 3145728 | tf_op jit(solution)/shard_map/order/pallas_call | solution.py:167
  5.0 0.0 copy-done.1
  5.0 0.0 copy-start.3
  5.0 0.0 copy-start.4
  5.0 19.8 %pad.1.padded_ref = f32[2,512,512]{2,1,0:T(8,128)S(1)} custom-call(f32[2,256,256]{2,1,0:T(8,128)S(1)} %copy-done.1), custom_call_target="tpu_custom_call" | custom-call | tf_op jit(solution)/shard_map/pad/pallas_call | solution.py:463
  24.9 0.0 copy-done.3
  24.9 0.0 copy-done.4
  24.9 6.7 %slots.2.grad_ref = f32[2,512,512]{2,1,0:T(8,128)S(1)} custom-call(s32[1,1,6,2]{3,2,1,0:T(8,128)S(1)} %copy.9.positions_ref, s32[1,1]{1,0:T(1,128)S(6)} %copy.11.counts_ref, f32[2,512,512]{2,1,0:T(8,128)S(1)} %pad.1.padded_ref, f32[2,256,256]{2,1,0:T(8,128)S(1)} %copy-done.3, f32[6,256,256]{2,1,0:T(8,128)S(1)} %order.1.measured_ref, ...), custom_call_target="tpu_custom_call" | custom-call | flops 4831838208 | bytes 15728640 | tf_op jit(solution)/shard_map/slots/pallas_call | solution.py:182
  31.6 34.1 %step.2.padded_ref = f32[2,512,512]{2,1,0:T(8,128)S(1)} custom-call(f32[2,512,512]{2,1,0:T(8,128)S(1)} %slots.2.grad_ref, f32[2,512,512]{2,1,0:T(8,128)S(1)} %pad.1.padded_ref), custom_call_target="tpu_custom_call" | custom-call | tf_op jit(solution)/shard_map/step/pallas_call | solution.py:463
  65.7 6.7 %slots.3.grad_ref = f32[2,512,512]{2,1,0:T(8,128)S(1)} custom-call(s32[1,1,6,2]{3,2,1,0:T(8,128)S(1)} %copy.9.positions_ref, s32[1,1]{1,0:T(1,128)S(6)} %copy.11.counts_ref, f32[2,512,512]{2,1,0:T(8,128)S(1)} %step.2.padded_ref, f32[2,256,256]{2,1,0:T(8,128)S(1)} %copy-done.3, f32[6,256,256]{2,1,0:T(8,128)S(1)} %order.1.measured_ref, ...), custom_call_target="tpu_custom_call" | custom-call | flops 4831838208 | bytes 15728640 | tf_op jit(solution)/shard_map/slots/pallas_call | solution.py:182
  72.4 18.8 %step.3 = f32[2,256,256]{2,1,0:T(8,128)S(1)} custom-call(f32[2,512,512]{2,1,0:T(8,128)S(1)} %slots.3.grad_ref, f32[2,512,512]{2,1,0:T(8,128)S(1)} %step.2.padded_ref), custom_call_target="tpu_custom_call" | custom-call | tf_op jit(solution)/shard_map/step/pallas_call | solution.py:463
  91.2 0.8 copy.12
Async XLA Ops:
  1.4 1.4 %copy-start = (s32[1,1,6,256,256]{4,3,2,1,0:T(8,128)S(1)}, s32[1,1,6,256,256]{4,3,2,1,0:T(8,128)}, u32[]{:S(2)}) copy-start(s32[1,1,6,256,256]{4,3,2,1,0:T(8,128)} %param.11) | copy-start | bytes 4718596
  2.8 0.9 %copy-start.2 = (bf16[2,256,256]{2,1,0:T(8,128)(2,1)S(1)}, bf16[2,256,256]{2,1,0:T(8,128)(2,1)}, u32[]{:S(2)}) copy-start(bf16[2,256,256]{2,1,0:T(8,128)(2,1)} %constant.5.clone.order_ref) | copy-start | bytes 786436
  3.8 1.2 %copy-start.1 = (f32[2,256,256]{2,1,0:T(8,128)S(1)}, f32[2,256,256]{2,1,0:T(8,128)}, u32[]{:S(2)}) copy-start(f32[2,256,256]{2,1,0:T(8,128)} %field_ref.1) | copy-start | bytes 1572868
  5.0 19.8 %copy-start.3 = (f32[2,256,256]{2,1,0:T(8,128)S(1)}, f32[2,256,256]{2,1,0:T(8,128)}, u32[]{:S(2)}) copy-start(f32[2,256,256]{2,1,0:T(8,128)} %probe_ref.3) | copy-start | bytes 1572868
  5.0 19.8 %copy-start.4 = (bf16[2,4,256,256]{3,2,1,0:T(8,128)(2,1)S(1)}, bf16[2,4,256,256]{3,2,1,0:T(8,128)(2,1)}, u32[]{:S(2)}) copy-start(bf16[2,4,256,256]{3,2,1,0:T(8,128)(2,1)} %constant.4.clone.table_ref) | copy-start | bytes 3145732

commit v2 on v1

--- a/solution.py
+++ b/solution.py
@@ -12,6 +12,7 @@
 ITERS = 2
 LANES = 128
 ROWS = 8
+PAIR = 2
 
 
 step_rate = 0.02
@@ -35,15 +36,6 @@
     return np.stack([high, low])
 
 
-def ordering(length):
-    half = length // 2
-    index = np.arange(half)
-    table = np.zeros((length, length), np.float32)
-    table[2 * index, index] = 1
-    table[2 * index + 1, half + index] = 1
-    return np.stack([table, table.T]).astype(jnp.bfloat16)
-
-
 def dot(left, right):
     return lax.dot_general(left, right, (((1,), (0,)), ((), ())), preferred_element_type=jnp.float32)
 
@@ -53,128 +45,157 @@
     return high, (value - high.astype(jnp.float32)).astype(jnp.bfloat16)
 
 
+def order_columns(length):
+    half = length // 2
+    here = lax.broadcasted_iota(jnp.int32, (length, length), 0)
+    there = lax.broadcasted_iota(jnp.int32, (length, length), 1)
+    wanted = jnp.where(there < half, 2 * there, 2 * there - length + 1)
+    return jnp.where(here == wanted, 1.0, 0.0).astype(jnp.bfloat16)
+
+
+def put_in_order(raw_ref, measured_ref, order):
+    parts, size, _ = raw_ref.shape
+    given = jnp.concatenate(
+        [
+            jnp.concatenate([raw_ref[c, pl.ds(odd, size // 2, stride=2)] for c in range(parts)], axis=1)
+            for odd in (0, 1)
+        ],
+        axis=0,
+    )
+
+    def placed(value):
+        return dot(value.astype(jnp.float32).astype(jnp.bfloat16), order)
+
+    measured_ref[...] = (placed(given >> 4) * 16.0 + placed(given & 15)) * photon_unit
+
+
 def from_left(table, which, value):
-    high, low = parted(value)
-    return dot(table[0, which], high) + dot(table[1, which], high) + dot(table[0, which], low)
+    high, low = value
+    table = jnp.concatenate([table[0, which], table[1, which], table[0, which]], axis=1)
+    return dot(table, jnp.concatenate([high, high, low], axis=0))
 
 
 def from_right(table, which, value):
-    high, low = parted(value)
-    return dot(high, table[0, which]) + dot(high, table[1, which]) + dot(low, table[0, which])
-
-
-def order_kernel(counts_ref, order_ref, intensity_ref, out_ref):
-    @pl.loop(0, counts_ref[0, 0])
-    def _(slot):
-        given = intensity_ref[slot]
-
-        def placed(value):
-            value = value.astype(jnp.float32).astype(jnp.bfloat16)
-            return dot(dot(order_ref[1], value).astype(jnp.bfloat16), order_ref[0])
-
-        out_ref[slot] = (placed(given >> 4) * 16.0 + placed(given & 15)) * photon_unit
-
-
-def moved_up(value, shift):
+    high, low = value
+    table = jnp.concatenate([table[0, which], table[1, which], table[0, which]], axis=0)
+    return dot(jnp.concatenate([high, high, low], axis=1), table)
+
+
+def turned(value, drop, shift):
     rows, columns = value.shape
-    groups = value.reshape(rows // ROWS, ROWS, columns)
-    turned = pltpu.roll(groups, (ROWS - shift) % ROWS, 1)
-    within = lax.broadcasted_iota(jnp.int32, (1, ROWS, columns), 1) < ROWS - shift
-    return jnp.where(within, turned[:-1], turned[1:]).reshape(rows - ROWS, columns)
-
-
-def moved_down(value, shift):
-    rows, columns = value.shape
-    groups = value.reshape(rows // ROWS, ROWS, columns)
-    turned = pltpu.roll(groups, shift % ROWS, 1)
-    none = jnp.zeros((1, ROWS, columns), value.dtype)
-    within = lax.broadcasted_iota(jnp.int32, (1, ROWS, columns), 1) >= shift
-    lower = jnp.concatenate([turned, none], axis=0)
-    upper = jnp.concatenate([none, turned], axis=0)
-    return jnp.where(within, lower, upper).reshape(rows + ROWS, columns)
-
-
-def moved_left(value, shift):
-    rows, columns = value.shape
-    parts = [pltpu.roll(value[:, c : c + LANES], (LANES - shift) % LANES, 1) for c in range(0, columns, LANES)]
-    within = lax.broadcasted_iota(jnp.int32, (rows, LANES), 1) < LANES - shift
-    return jnp.concatenate([jnp.where(within, a, b) for a, b in zip(parts[:-1], parts[1:])], axis=1)
-
-
-def moved_right(value, shift):
-    rows, columns = value.shape
+    groups = pltpu.roll(value.reshape(rows // ROWS, ROWS, columns), drop % ROWS, 1)
+    before = jnp.concatenate([groups[-1:], groups[:-1]], axis=0)
+    within = lax.broadcasted_iota(jnp.int32, (1, ROWS, columns), 1) >= drop
+    value = jnp.where(within, groups, before).reshape(rows, columns)
     parts = [pltpu.roll(value[:, c : c + LANES], shift % LANES, 1) for c in range(0, columns, LANES)]
     within = lax.broadcasted_iota(jnp.int32, (rows, LANES), 1) >= shift
-    none = jnp.zeros((rows, LANES), value.dtype)
-    return jnp.concatenate([jnp.where(within, a, b) for a, b in zip(parts + [none], [none] + parts)], axis=1)
-
-
-def slots_kernel(positions_ref, counts_ref, padded_ref, probe_ref, measured_ref, table_ref, grad_ref):
+    return jnp.concatenate([jnp.where(within, a, b) for a, b in zip(parts, parts[-1:] + parts[:-1])], axis=1)
+
+
+def wrapped(value, drop, shift):
+    rows, columns = value.shape[0] - ROWS, value.shape[1] - LANES
+    below = lax.broadcasted_iota(jnp.int32, (ROWS, columns + LANES), 0) >= drop
+    value = jnp.concatenate([jnp.where(below, value[:ROWS], value[rows:]), value[ROWS:rows]], axis=0)
+    beside = lax.broadcasted_iota(jnp.int32, (rows, LANES), 1) >= shift
+    return jnp.concatenate([jnp.where(beside, value[:, :LANES], value[:, columns:]), value[:, LANES:columns]], axis=1)
+
+
+def unwrapped(value, drop, shift):
+    rows, columns = value.shape
+    head = value[:, :LANES]
+    none = jnp.zeros_like(head)
+    beside = lax.broadcasted_iota(jnp.int32, (rows, LANES), 1) >= shift
+    value = jnp.concatenate(
+        [jnp.where(beside, head, none), value[:, LANES:], jnp.where(beside, none, head)], axis=1
+    )
+    head = value[:ROWS]
+    none = jnp.zeros_like(head)
+    below = lax.broadcasted_iota(jnp.int32, (ROWS, columns + LANES), 0) >= drop
+    return jnp.concatenate(
+        [jnp.where(below, head, none), value[ROWS:], jnp.where(below, none, head)], axis=0
+    )
+
+
+def slot_stages(slot, positions_ref, padded_ref, probe_ref, measured_ref, table_ref, grad_ref):
     size = probe_ref.shape[1]
     half = size // 2
-    wide = size + LANES
     last = padded_ref.shape[1] - size - ROWS
+    row = positions_ref[0, slot]
+    column = positions_ref[1, slot]
+    start = pl.multiple_of(jnp.where(column >= LANES, LANES, 0), LANES)
+    shift = column - start
+    first = pl.multiple_of(jnp.minimum(row // ROWS * ROWS, last), ROWS)
+    drop = row - first
+    there = (pl.ds(first, size + ROWS), pl.ds(start, size + LANES))
+    probe_r = turned(probe_ref[0], drop, shift)
+    probe_i = turned(probe_ref[1], drop, shift)
+    yield
+    patch_r = wrapped(padded_ref[(0, *there)], drop, shift)
+    patch_i = wrapped(padded_ref[(1, *there)], drop, shift)
+    exit_r = probe_r * patch_r - probe_i * patch_i
+    exit_i = probe_r * patch_i + probe_i * patch_r
+    upper = jnp.concatenate([exit_r[:half], exit_i[:half]], axis=0)
+    lower = jnp.concatenate([exit_r[half:], exit_i[half:]], axis=0)
+    even, odd = parted(upper + lower), parted(upper - lower)
+    yield
+    even, odd = from_left(table_ref, 0, even), from_left(table_ref, 2, odd)
+    yield
+    half_r = jnp.concatenate([even[:half], odd[:half]], axis=0)
+    half_i = jnp.concatenate([even[half:], odd[half:]], axis=0)
+    left = jnp.concatenate([half_r[:, :half], half_i[:, :half]], axis=1)
+    right = jnp.concatenate([half_r[:, half:], half_i[:, half:]], axis=1)
+    values = [parted(left + right), parted(left - right)]
+    yield
+    specs = [from_right(table_ref, 2 * odd + 1, value) for odd, value in enumerate(values)]
+    yield
+    values = []
+    for odd, spec in enumerate(specs):
+        spec_r, spec_i = spec[:, :half], spec[:, half:]
+        misfit = spec_r * spec_r + spec_i * spec_i - measured_ref[slot, :, odd * half : (odd + 1) * half]
+        values.append(parted(jnp.concatenate([misfit * spec_r, misfit * spec_i], axis=1)))
+    yield
+    backs = [from_right(table_ref, 2 * odd, value) for odd, value in enumerate(values)]
+    yield
+    left = backs[0] + backs[1]
+    right = backs[0] - backs[1]
+    half_r = jnp.concatenate([left[:, :half], right[:, :half]], axis=1)
+    half_i = jnp.concatenate([left[:, half:], right[:, half:]], axis=1)
+    even = parted(jnp.concatenate([half_r[:half], half_i[:half]], axis=0))
+    odd = parted(jnp.concatenate([half_r[half:], half_i[half:]], axis=0))
+    yield
+    even, odd = from_left(table_ref, 1, even), from_left(table_ref, 3, odd)
+    yield
+    upper = even + odd
+    lower = even - odd
+    back_r = jnp.concatenate([upper[:half], lower[:half]], axis=0)
+    back_i = jnp.concatenate([upper[half:], lower[half:]], axis=0)
+    term_r = probe_r * back_r + probe_i * back_i
+    term_i = probe_r * back_i - probe_i * back_r
+    for part, term in ((0, term_r), (1, term_i)):
+        grad_ref[(part, *there)] += unwrapped(term, drop, shift)
+
+
+def side_by_side(works):
+    works = list(works)
+    while works:
+        works = [work for work in works if next(work, works) is not works]
+
+
+def slots_kernel(positions_ref, counts_ref, padded_ref, *refs):
+    grad_ref = refs[-1]
+    count = counts_ref[0, 0]
     grad_ref[...] = jnp.zeros_like(grad_ref)
 
-    @pl.loop(0, counts_ref[0, 0])
+    def work(slot):
+        return slot_stages(slot, positions_ref, padded_ref, *refs)
+
+    @pl.loop(0, count // PAIR)
+    def _(group):
+        side_by_side(work(group * PAIR + k) for k in range(PAIR))
+
+    @pl.loop(count // PAIR * PAIR, count)
     def _(slot):
-        row = positions_ref[0, 0, slot, 0]
-        column = positions_ref[0, 0, slot, 1]
-        start = pl.multiple_of(jnp.where(column >= LANES, LANES, 0), LANES)
-        shift = column - start
-        first = pl.multiple_of(jnp.minimum(row // ROWS * ROWS, last), ROWS)
-        drop = row - first
-        there = (pl.ds(first, size + ROWS), pl.ds(start, wide))
-        patch_r = moved_left(moved_up(padded_ref[(0, *there)], drop), shift)
-        patch_i = moved_left(moved_up(padded_ref[(1, *there)], drop), shift)
-        probe_r = probe_ref[0]
-        probe_i = probe_ref[1]
-        exit_r = probe_r * patch_r - probe_i * patch_i
-        exit_i = probe_r * patch_i + probe_i * patch_r
-        upper = jnp.concatenate([exit_r[:half], exit_i[:half]], axis=0)
-        lower = jnp.concatenate([exit_r[half:], exit_i[half:]], axis=0)
-        even = from_left(table_ref, 0, upper + lower)
-        odd = from_left(table_ref, 2, upper - lower)
-        half_r = jnp.concatenate([even[:half], odd[:half]], axis=0)
-        half_i = jnp.concatenate([even[half:], odd[half:]], axis=0)
-        left = jnp.concatenate([half_r[:, :half], half_i[:, :half]], axis=1)
-        right = jnp.concatenate([half_r[:, half:], half_i[:, half:]], axis=1)
-        backs = []
-        for odd, value in ((0, left + right), (1, left - right)):
-            spec = from_right(table_ref, 2 * odd + 1, value)
-            spec_r, spec_i = spec[:, :half], spec[:, half:]
-            misfit = spec_r * spec_r + spec_i * spec_i - measured_ref[slot, :, odd * half : (odd + 1) * half]
-            scaled = jnp.concatenate([misfit * spec_r, misfit * spec_i], axis=1)
-            backs.append(from_right(table_ref, 2 * odd, scaled))
-        left = backs[0] + backs[1]
-        right = backs[0] - backs[1]
-        half_r = jnp.concatenate([left[:, :half], right[:, :half]], axis=1)
-        half_i = jnp.concatenate([left[:, half:], right[:, half:]], axis=1)
-        even = from_left(table_ref, 1, jnp.concatenate([half_r[:half], half_i[:half]], axis=0))
-        odd = from_left(table_ref, 3, jnp.concatenate([half_r[half:], half_i[half:]], axis=0))
-        upper = even + odd
-        lower = even - odd
-        back_r = jnp.concatenate([upper[:half], lower[:half]], axis=0)
-        back_i = jnp.concatenate([upper[half:], lower[half:]], axis=0)
-        term_r = probe_r * back_r + probe_i * back_i
-        term_i = probe_r * back_i - probe_i * back_r
-        for part, term in ((0, term_r), (1, term_i)):
-            grad_ref[(part, *there)] += moved_down(moved_right(term, shift), drop)
-
-
-def in_order(counts, intensity, order):
-    slots, size, _ = intensity.shape
-    return pl.pallas_call(
-        order_kernel,
-        out_shape=jax.ShapeDtypeStruct((slots, size, size), jnp.float32),
-        in_specs=[pl.BlockSpec(memory_space=pltpu.SMEM)] + [pl.BlockSpec(memory_space=pltpu.VMEM)] * 2,
-        out_specs=pl.BlockSpec(memory_space=pltpu.VMEM),
-        cost_estimate=pl.CostEstimate(
-            flops=slots * 4 * size**3, bytes_accessed=slots * 8 * size**2, transcendentals=0
-        ),
-        compiler_params=pltpu.CompilerParams(vmem_limit_bytes=12 * 1024 * 1024),
-        name="order",
-    )(counts, order, intensity)
+        side_by_side([work(slot)])
 
 
 def slot_terms(positions, counts, padded, probe, measured, table):
@@ -295,9 +316,24 @@
     return jnp.logical_not(flag)
 
 
-def pad_kernel(field_ref, out_ref, relay_ref, send_sems, recv_sems):
+def pad_kernel(
+    field_ref, intensity_ref, out_ref, measured_ref, relay_ref, raw_ref, send_sems, recv_sems, local_sems
+):
     m = MARGIN
     planes, high, wide = field_ref.shape
+    slots, size, _ = measured_ref.shape
+    own = pltpu.make_async_copy(field_ref, out_ref.at[:, pl.ds(m, high), pl.ds(m, wide)], local_sems.at[slots * (size // LANES)])
+    own.start()
+    parts = size // LANES
+    fetches = [
+        pltpu.make_async_copy(
+            intensity_ref.at[0, 0, k, :, pl.ds(c * LANES, LANES)], raw_ref.at[k, c], local_sems.at[k * parts + c]
+        )
+        for k in range(slots)
+        for c in range(parts)
+    ]
+    for fetch in fetches:
+        fetch.start()
     around = Around(send_sems, recv_sems)
     here = around.here
     around.meet()
@@ -326,7 +362,6 @@
     for p in range(planes):
         for d in (-1, 1):
             cols[p, d].start()
-    out_ref[:, m : m + high, m : m + wide] = field_ref[...]
     for v in (-1, 1):
 
         @pl.when(no(here["rows", v]))
@@ -347,6 +382,11 @@
         def _():
             out_ref[:, m : m + high, land] = jnp.zeros((planes, high, m), jnp.float32)
 
+    order = order_columns(size)
+    for k in range(slots):
+        for c in range(parts):
+            fetches[k * parts + c].wait()
+        put_in_order(raw_ref.at[k], measured_ref.at[k], order)
     if around.relays:
         for d in (-1, 1):
             rows[0, d].forward()
@@ -366,6 +406,7 @@
             cols[p, d].wait_send()
             for v in (-1, 1):
                 pl.when(both(here["rows", v], here["cols", d]))(corners[p, v, d].wait_send)
+    own.wait()
 
 
 def step_kernel(last, grad_ref, padded_ref, out_ref, mid_ref, side_ref, band_ref, relay_ref, send_sems, recv_sems):
@@ -474,17 +515,41 @@
     )(*arrays)
 
 
+def pad_and_order(field, intensity, relay):
+    planes, high, wide = field.shape
+    slots, size, _ = intensity.shape[2:]
+    copies = 16 * planes
+    return pl.pallas_call(
+        pad_kernel,
+        out_shape=[
+            jax.ShapeDtypeStruct((planes, high + 2 * MARGIN, wide + 2 * MARGIN), jnp.float32),
+            jax.ShapeDtypeStruct((slots, size, size), jnp.float32),
+        ],
+        in_specs=[pl.BlockSpec(memory_space=pltpu.HBM)] * 2,
+        out_specs=[pl.BlockSpec(memory_space=pltpu.VMEM)] * 2,
+        scratch_shapes=[
+            pltpu.VMEM(relay, jnp.float32),
+            pltpu.VMEM((slots, size // LANES, size, LANES), jnp.int32),
+            pltpu.SemaphoreType.DMA((copies,)),
+            pltpu.SemaphoreType.DMA((copies,)),
+            pltpu.SemaphoreType.DMA((slots * (size // LANES) + 1,)),
+        ],
+        compiler_params=pltpu.CompilerParams(
+            collective_id=0, has_side_effects=True, vmem_limit_bytes=16 * 1024 * 1024
+        ),
+        name="pad",
+    )(*(pltpu.with_memory_space_constraint(array, pltpu.HBM) for array in (field, intensity)))
+
+
 def on_device(object_field, probe, positions, counts, intensity):
     planes, high, wide = object_field.shape
-    size = probe.shape[1]
-    table = jnp.asarray(tables(size))
-    order = jnp.asarray(ordering(size))
-    measured = in_order(counts, intensity[0, 0], order)
+    table = jnp.asarray(tables(probe.shape[1]))
+    positions = positions[0, 0].T
     tall, broad = high + 2 * MARGIN, wide + 2 * MARGIN
     outer = (planes, tall, broad)
     relay = (planes, 2, MARGIN, wide)
     scratch = [(planes, tall, wide), (2, planes, tall, MARGIN), (planes, tall, wide), relay]
-    padded = exchange(pad_kernel, "pad", 0, outer, [relay], 16 * planes, object_field)
+    padded, measured = pad_and_order(object_field, intensity, relay)
     for step in range(ITERS):
         grad = slot_terms(positions, counts, padded, probe, measured, table)
         last = step == ITERS - 1

time: 93.9 us -> 81 us (0.86); the launches traced: 92 us -> 81 us
  Pallas kernels: 87.3 us -> 79.3 us
  local copies, waits for them, and re-layouts: 3.94 us -> 0.81 us
    pallas_call x3 -> x2, Pallas kernels: 72.7 us -> 43.1 us  [exchange(): pl.pallas_call(kernel, out_shape=jax.ShapeDtypeStruct(shape, jnp.float32)...]
    pallas_call x1, Pallas kernels: 1.22 us -> 19.3 us  [pad_and_order(): pl.pallas_call(pad_kernel, out_shape=[jax.ShapeDtypeStruct((planes, high...]
    pallas_call x2, Pallas kernels: 13.5 us -> 16.9 us  [slot_terms(): pl.pallas_call(slots_kernel, out_shape=jax.ShapeDtypeStruct(padded.shape,...]
    unnamed x12 -> x7, local copies, waits for them, and re-layouts: 3.94 us -> 0.81 us
where the time goes in v2:
time: 81 us
  Pallas kernels  79.3 us (98%)
  between operations  0.84 us (1%)
  local copies, waits for them, and re-layouts  0.81 us (1%)
    pallas_call x2, Pallas kernels, exchange(): pl.pallas_call(kernel, out_shape=jax.ShapeDtypeStruct(shape, jnp.float32)...  43.1 us
    pallas_call x1, Pallas kernels, pad_and_order(): pl.pallas_call(pad_kernel, out_shape=[jax.ShapeDtypeStruct((planes, high...  19.3 us
    pallas_call x2, Pallas kernels, slot_terms(): pl.pallas_call(slots_kernel, out_shape=jax.ShapeDtypeStruct(padded.shape,...  16.9 us

profile of v2, /device:TPU:5, one launch (start us, length us, event | category | flops | bytes accessed | tf_op | source)
XLA Modules:
  0.0 81.0 jit_solution(5697078070001047496)
XLA Ops:
  0.0 0.0 copy-start.2
  0.0 0.0 copy-start
  0.0 0.0 copy-start.1
  0.8 19.3 %pad.1 = (f32[2,512,512]{2,1,0:T(8,128)S(1)}, f32[6,256,256]{2,1,0:T(8,128)S(1)}) custom-call(f32[2,256,256]{2,1,0:T(8,128)} %field_ref.1, s32[1,1,6,256,256]{4,3,2,1,0:T(8,128)} %intensity_ref.1), custom_call_target="tpu_custom_call" | custom-call | tf_op jit(solution)/shard_map/pad/pallas_call | solution.py:522
  20.1 0.0 copy-done.2
  20.1 0.0 copy-done
  20.1 0.0 copy-done.1
  20.1 8.4 %slots.2.grad_ref = f32[2,512,512]{2,1,0:T(8,128)S(1)} custom-call(s32[2,6]{1,0:T(2,128)S(1)} %bitcast.3, s32[1,1]{1,0:T(1,128)S(6)} %copy.8.counts_ref, f32[2,512,512]{2,1,0:T(8,128)S(1)} %get-tuple-element.7.padded_ref, f32[2,256,256]{2,1,0:T(8,128)S(1)} %copy-done, f32[6,256,256]{2,1,0:T(8,128)S(1)} %get-tuple-element.8.refs_1_, ...), custom_call_target="tpu_custom_call" | custom-call | flops 4831838208 | bytes 15728640 | tf_op jit(solution)/shard_map/slots/pallas_call | solution.py:203
  28.6 28.6 %step.2.padded_ref = f32[2,512,512]{2,1,0:T(8,128)S(1)} custom-call(f32[2,512,512]{2,1,0:T(8,128)S(1)} %slots.2.grad_ref, f32[2,512,512]{2,1,0:T(8,128)S(1)} %get-tuple-element.7.padded_ref), custom_call_target="tpu_custom_call" | custom-call | tf_op jit(solution)/shard_map/step/pallas_call | solution.py:504
  57.1 8.4 %slots.3.grad_ref = f32[2,512,512]{2,1,0:T(8,128)S(1)} custom-call(s32[2,6]{1,0:T(2,128)S(1)} %bitcast.4, s32[1,1]{1,0:T(1,128)S(6)} %copy.8.counts_ref, f32[2,512,512]{2,1,0:T(8,128)S(1)} %step.2.padded_ref, f32[2,256,256]{2,1,0:T(8,128)S(1)} %copy-done, f32[6,256,256]{2,1,0:T(8,128)S(1)} %get-tuple-element.8.refs_1_, bf16[2,4,256,256]{3,2,1,0:T(8,128)(2,1)S(1)} %copy-done.2), custom_call_target="tpu_custom_call" | custom-call | flops 4831838208 | bytes 15728640 | tf_op jit(solution)/shard_map/slots/pallas_call | solution.py:203
  65.6 14.6 %step.3 = f32[2,256,256]{2,1,0:T(8,128)S(1)} custom-call(f32[2,512,512]{2,1,0:T(8,128)S(1)} %slots.3.grad_ref, f32[2,512,512]{2,1,0:T(8,128)S(1)} %step.2.padded_ref), custom_call_target="tpu_custom_call" | custom-call | tf_op jit(solution)/shard_map/step/pallas_call | solution.py:504
  80.2 0.8 copy.9
Async XLA Ops:
  0.0 20.1 %copy-start.2 = (bf16[2,4,256,256]{3,2,1,0:T(8,128)(2,1)S(1)}, bf16[2,4,256,256]{3,2,1,0:T(8,128)(2,1)}, u32[]{:S(2)}) copy-start(bf16[2,4,256,256]{3,2,1,0:T(8,128)(2,1)} %constant.2.clone.refs_2_) | copy-start | bytes 3145732
  0.0 20.1 %copy-start = (f32[2,256,256]{2,1,0:T(8,128)S(1)}, f32[2,256,256]{2,1,0:T(8,128)}, u32[]{:S(2)}) copy-start(f32[2,256,256]{2,1,0:T(8,128)} %refs_0_.3) | copy-start | bytes 1572868
  0.0 20.1 %copy-start.1 = (s32[1,1,6,2]{2,3,1,0:T(2,128)S(1)}, s32[1,1,6,2]{2,3,1,0:T(2,128)}, u32[]{:S(2)}) copy-start(s32[1,1,6,2]{2,3,1,0:T(2,128)} %param.8) | copy-start | bytes 148

commit v3 on v2

v3 whole, which is shorter than its diff:
```python
import functools
import itertools

import jax
import jax.numpy as jnp
import numpy as np
from jax import lax
from jax.experimental import pallas as pl
from jax.experimental.pallas import tpu as pltpu
from jax.sharding import PartitionSpec as P

MARGIN = 128
ITERS = 2
LANES = 128
ROWS = 8
PAIR = 2
BLOCKS = 4


step_rate = 0.02
photon_unit = 0.001


def tables(length):
    half = length // 2
    k = np.arange(half)[:, None]
    n = np.arange(half)[None, :]
    found = []
    for odd in (0, 1):
        angle = ((2 * k + odd) * n % length) * (2.0 * np.pi / length)
        c = np.cos(angle) / np.sqrt(length)
        s = np.sin(angle) / np.sqrt(length)
        full = np.block([[c, s], [-s, c]])
        found += [full, full.T]
    full = np.stack(found).astype(np.float32)
    high = full.astype(jnp.bfloat16)
    low = (full - high.astype(np.float32)).astype(jnp.bfloat16)
    return np.stack([high, low])


def dot(left, right):
    return lax.dot_general(left, right, (((1,), (0,)), ((), ())), preferred_element_type=jnp.float32)


def parted(value):
    high = value.astype(jnp.bfloat16)
    return high, (value - high.astype(jnp.float32)).astype(jnp.bfloat16)


def order_columns(length):
    half = length // 2
    here = lax.broadcasted_iota(jnp.int32, (length, length), 0)
    there = lax.broadcasted_iota(jnp.int32, (length, length), 1)
    wanted = jnp.where(there < half, 2 * there, 2 * there - length + 1)
    return jnp.where(here == wanted, 1.0, 0.0).astype(jnp.bfloat16)


def put_in_order(raw_ref, measured_ref, order):
    parts, size, _ = raw_ref.shape
    given = jnp.concatenate(
        [
            jnp.concatenate([raw_ref[c, pl.ds(odd, size // 2, stride=2)] for c in range(parts)], axis=1)
            for odd in (0, 1)
        ],
        axis=0,
    )

    def placed(value):
        return dot(value.astype(jnp.float32).astype(jnp.bfloat16), order)

    measured_ref[...] = (placed(given >> 4) * 16.0 + placed(given & 15)) * photon_unit


def from_left(table, which, value):
    high, low = value
    table = jnp.concatenate([table[0, which], table[1, which], table[0, which]], axis=1)
    return dot(table, jnp.concatenate([high, high, low], axis=0))


def from_right(table, which, value):
    high, low = value
    table = jnp.concatenate([table[0, which], table[1, which], table[0, which]], axis=0)
    return dot(jnp.concatenate([high, high, low], axis=1), table)


def turned(value, drop, shift):
    rows, columns = value.shape
    groups = pltpu.roll(value.reshape(rows // ROWS, ROWS, columns), drop % ROWS, 1)
    before = jnp.concatenate([groups[-1:], groups[:-1]], axis=0)
    within = lax.broadcasted_iota(jnp.int32, (1, ROWS, columns), 1) >= drop
    value = jnp.where(within, groups, before).reshape(rows, columns)
    parts = [pltpu.roll(value[:, c : c + LANES], shift % LANES, 1) for c in range(0, columns, LANES)]
    within = lax.broadcasted_iota(jnp.int32, (rows, LANES), 1) >= shift
    return jnp.concatenate([jnp.where(within, a, b) for a, b in zip(parts, parts[-1:] + parts[:-1])], axis=1)


def slot_stages(slot, positions_ref, padded_ref, probes_ref, measured_ref, table_ref, terms):
    size = probes_ref.shape[2]
    half = size // 2
    below = lax.broadcasted_iota(jnp.int32, (size, size), 0) >= positions_ref[0, slot]
    beside = lax.broadcasted_iota(jnp.int32, (size, size), 1) >= positions_ref[1, slot]

    def folded(p):
        upper = jnp.where(beside, padded_ref[p, :size, :size], padded_ref[p, :size, size:])
        lower = jnp.where(beside, padded_ref[p, size:, :size], padded_ref[p, size:, size:])
        return jnp.where(below, upper, lower)

    probe_r = probes_ref[slot, 0]
    probe_i = probes_ref[slot, 1]
    patch_r, patch_i = folded(0), folded(1)
    exit_r = probe_r * patch_r - probe_i * patch_i
    exit_i = probe_r * patch_i + probe_i * patch_r
    upper = jnp.concatenate([exit_r[:half], exit_i[:half]], axis=0)
    lower = jnp.concatenate([exit_r[half:], exit_i[half:]], axis=0)
    even, odd = parted(upper + lower), parted(upper - lower)
    yield
    even, odd = from_left(table_ref, 0, even), from_left(table_ref, 2, odd)
    yield
    half_r = jnp.concatenate([even[:half], odd[:half]], axis=0)
    half_i = jnp.concatenate([even[half:], odd[half:]], axis=0)
    left = jnp.concatenate([half_r[:, :half], half_i[:, :half]], axis=1)
    right = jnp.concatenate([half_r[:, half:], half_i[:, half:]], axis=1)
    values = [parted(left + right), parted(left - right)]
    yield
    specs = [from_right(table_ref, 2 * odd + 1, value) for odd, value in enumerate(values)]
    yield
    values = []
    for odd, spec in enumerate(specs):
        spec_r, spec_i = spec[:, :half], spec[:, half:]
        misfit = spec_r * spec_r + spec_i * spec_i - measured_ref[slot, :, odd * half : (odd + 1) * half]
        values.append(parted(jnp.concatenate([misfit * spec_r, misfit * spec_i], axis=1)))
    yield
    backs = [from_right(table_ref, 2 * odd, value) for odd, value in enumerate(values)]
    yield
    left = backs[0] + backs[1]
    right = backs[0] - backs[1]
    half_r = jnp.concatenate([left[:, :half], right[:, :half]], axis=1)
    half_i = jnp.concatenate([left[:, half:], right[:, half:]], axis=1)
    even = parted(jnp.concatenate([half_r[:half], half_i[:half]], axis=0))
    odd = parted(jnp.concatenate([half_r[half:], half_i[half:]], axis=0))
    yield
    even, odd = from_left(table_ref, 1, even), from_left(table_ref, 3, odd)
    yield
    upper = even + odd
    lower = even - odd
    back_r = jnp.concatenate([upper[:half], lower[:half]], axis=0)
    back_i = jnp.concatenate([upper[half:], lower[half:]], axis=0)
    term_r = probe_r * back_r + probe_i * back_i
    term_i = probe_r * back_i - probe_i * back_r
    for term in (term_r, term_i):
        upper, lower = jnp.where(below, term, 0.0), jnp.where(below, 0.0, term)
        terms.append([jnp.where(beside, t, 0.0) if left else jnp.where(beside, 0.0, t) for t in (upper, lower) for left in (1, 0)])


def side_by_side(works):
    works = list(works)
    while works:
        works = [work for work in works if next(work, works) is not works]


def turn_kernel(positions_ref, counts_ref, probe_ref, probes_ref, twice_ref):
    planes, size, _ = probe_ref.shape
    slots = probes_ref.shape[0]
    count = counts_ref[0, 0]

    @pl.loop(0, count)
    def _(slot):
        row = lax.rem(positions_ref[0, slot], size)
        column = lax.rem(positions_ref[1, slot], size)
        drop, shift = lax.rem(row, ROWS), lax.rem(column, LANES)
        first = pl.multiple_of(size - (row - drop), ROWS)
        for p in range(planes):
            value = turned(probe_ref[p], drop, shift)
            parts = [value[:, c : c + LANES] for c in range(0, size, LANES)]
            for k in range(1, size // LANES):
                moved = jnp.concatenate(parts[-k:] + parts[:-k], axis=1)
                value = jnp.where(column // LANES == k, moved, value)
            twice_ref[p, :size] = value
            twice_ref[p, size:] = value
            probes_ref[slot, p] = twice_ref[p, pl.ds(first, size)]

    @pl.loop(count, slots)
    def _(slot):
        probes_ref[slot] = jnp.zeros(probes_ref.shape[1:], jnp.float32)


def add_terms(positions_ref, padded_ref, probes_ref, measured_ref, table_ref, grad_ref):
    planes = padded_ref.shape[0]
    slots, size, _ = measured_ref.shape

    def group(begin, width):
        terms = [[] for _ in range(width)]
        side_by_side(
            slot_stages(begin + k, positions_ref, padded_ref, probes_ref, measured_ref, table_ref, terms[k])
            for k in range(width)
        )
        for p in range(planes):
            for k, (r, c) in enumerate(itertools.product((0, size), (0, size))):
                grad_ref[p, r : r + size, c : c + size] += sum(term[p][k] for term in terms)

    @pl.loop(0, slots // PAIR)
    def _(step):
        group(step * PAIR, PAIR)

    for slot in range(slots // PAIR * PAIR, slots):
        group(slot, 1)


MESH = pl.DeviceIdType.MESH


class Around:
    def __init__(self, send_sems, recv_sems):
        self.send_sems, self.recv_sems = send_sems, recv_sems
        self.sends = self.recvs = 0
        self.here, self.device = {}, {}
        for axis in ("rows", "cols"):
            count = lax.axis_size(axis)
            me = lax.axis_index(axis)
            for d in (-2, -1, 1, 2):
                self.here[axis, d] = me + d >= 0 if d < 0 else me + d < count
                self.device[axis, d] = {axis: lax.rem(me + count + d, count)}
        count = lax.axis_size("rows")
        self.relays = count > 2 and count % 2 == 0
        odd = lax.rem(lax.axis_index("rows"), 2) == 1
        self.far = {1: odd, -1: no(odd)}

    def meet(self):
        barrier = pltpu.get_barrier_semaphore()
        sides = [("rows", -1), ("rows", 1), ("cols", -1), ("cols", 1)]
        if self.relays:
            sides += [("rows", -2), ("rows", 2)]
        for side in sides:

            @pl.when(self.here[side])
            def _():
                pl.semaphore_signal(barrier, inc=1, device_id=self.device[side], device_id_type=MESH)

        pl.semaphore_wait(barrier, sum(self.here[side].astype(jnp.int32) for side in sides))

    def new_recv(self):
        self.recvs += 1
        return self.recvs - 1

    def copy(self, side, source, target, recv=None):
        recv = self.new_recv() if recv is None else recv
        self.sends += 1
        return pltpu.make_async_remote_copy(
            src_ref=source,
            dst_ref=target,
            send_sem=self.send_sems.at[self.sends - 1],
            recv_sem=self.recv_sems.at[recv],
            device_id=self.device[side],
            device_id_type=MESH,
        )


class Side:
    def __init__(self, around, axis, d, source, target):
        self.here, self.back = around.here[axis, d], around.here[axis, -d]
        self.straight = around.copy((axis, d), source, target)

    def start(self):
        pl.when(self.here)(self.straight.start)

    def forward(self):
        pass

    def wait_recv(self):
        pl.when(self.back)(self.straight.wait_recv)

    def wait_left(self):
        pl.when(self.here)(self.straight.wait_send)

    def wait_forwarded(self):
        pass


class Hop:
    def __init__(self, around, d, source, target, relay):
        here, far = around.here["rows", d], around.far[d]
        self.back = around.here["rows", -d]
        recv = around.new_recv()
        self.straight = around.copy(("rows", d), source, target, recv)
        self.near = both(here, no(far))
        self.long = both(here, far)
        self.middle = both(around.here["rows", -2 * d], far)
        self.first = around.copy(("rows", 2 * d), source, relay)
        self.second = around.copy(("rows", -d), relay, target, recv)

    def start(self):
        pl.when(self.near)(self.straight.start)
        pl.when(self.long)(self.first.start)

    def forward(self):
        @pl.when(self.middle)
        def _():
            self.first.wait_recv()
            self.second.start()

    def wait_recv(self):
        pl.when(self.back)(self.straight.wait_recv)

    def wait_left(self):
        pl.when(self.near)(self.straight.wait_send)
        pl.when(self.long)(self.first.wait_send)

    def wait_forwarded(self):
        pl.when(self.middle)(self.second.wait_send)


def both(first, second):
    return jnp.logical_and(first, second)


def no(flag):
    return jnp.logical_not(flag)


def pad(around, field_ref, out_ref, relay_ref, meanwhile):
    m = MARGIN
    planes, high, wide = field_ref.shape
    here = around.here
    part = m // 2
    row_from = {(-1, q): pl.ds(q * part, part) for q in (0, 1)} | {(1, q): pl.ds(high - m + q * part, part) for q in (0, 1)}
    row_land = {(1, q): pl.ds(q * part, part) for q in (0, 1)} | {(-1, q): pl.ds(m + high + q * part, part) for q in (0, 1)}
    col_cuts = {-1: (pl.ds(0, m), pl.ds(m + wide, m)), 1: (pl.ds(wide - m, m), pl.ds(0, m))}
    from_cuts = {-1: pl.ds(0, m), 1: pl.ds(m + high, m)}
    col_from = {-1: pl.ds(m, m), 1: pl.ds(wide, m)}
    rows, cols, corners = {}, {}, {}
    for d in (-1, 1):
        for q in (0, 1):
            source, target = field_ref.at[:, row_from[d, q]], out_ref.at[:, row_land[d, q], pl.ds(m, wide)]
            if around.relays and q == 0:
                rows[d, q] = Hop(around, d, source, target, relay_ref.at[0, :, pl.ds(0, part)])
            else:
                rows[d, q] = Side(around, "rows", d, source, target)
        cut, land = col_cuts[d]
        cols[d] = Side(around, "cols", d, field_ref.at[:, :, cut], out_ref.at[:, pl.ds(m, high), land])
        for v in (-1, 1):
            for q in (0, 1):
                lines = row_land[-v, q]
                corners[v, q, d] = around.copy(("cols", d), out_ref.at[:, lines, col_from[d]], out_ref.at[:, lines, land])
    for q in (0, 1):
        for d in (-1, 1):
            rows[d, q].start()
    for d in (-1, 1):
        cols[d].start()
    for v in (-1, 1):

        @pl.when(no(here["rows", v]))
        def _():
            out_ref[:, from_cuts[v], m : m + wide] = jnp.zeros((planes, m, wide), jnp.float32)

        for d in (-1, 1):
            land = col_cuts[-d][1]

            @pl.when(no(both(here["rows", v], here["cols", d])))
            def _():
                out_ref[:, from_cuts[v], land] = jnp.zeros((planes, m, m), jnp.float32)

    for d in (-1, 1):
        land = col_cuts[-d][1]

        @pl.when(no(here["cols", d]))
        def _():
            out_ref[:, m : m + high, land] = jnp.zeros((planes, high, m), jnp.float32)

    meanwhile()
    for d in (-1, 1):
        rows[d, 0].forward()
    for far in (-1, 1):

        @pl.when(around.far[far])
        def _():
            for v, q in ((-far, 0), (-far, 1), (far, 1), (far, 0)):
                rows[-v, q].wait_recv()
                for d in (-1, 1):
                    pl.when(both(here["rows", v], here["cols", d]))(corners[v, q, d].start)

    for d in (-1, 1):
        cols[-d].wait_recv()
        for v in (-1, 1):
            for q in (0, 1):
                pl.when(both(here["rows", v], here["cols", d]))(corners[v, q, -d].wait_recv)
    def rest():
        for copy in [*rows.values(), *cols.values()]:
            copy.wait_left()
            copy.wait_forwarded()
        for v, q, d in corners:
            pl.when(both(here["rows", v], here["cols", d]))(corners[v, q, d].wait_send)

    return rest


def step(last, around, grad_ref, padded_ref, out_ref, mid_ref, side_ref, band_ref, relay_ref):
    m = MARGIN
    planes, extent, _ = grad_ref.shape
    wide = extent - 2 * m
    part = extent // 2 // BLOCKS
    outside = m // part
    here = around.here
    begin = {(h, q): q * part if h < 0 else extent - (q + 1) * part for h in (-1, 1) for q in range(BLOCKS)}
    lines = {key: pl.ds(start, part) for key, start in begin.items()}
    cut = {-1: pl.ds(0, m), 1: pl.ds(extent - m, m)}
    inner = {-1: pl.ds(m, m), 1: pl.ds(wide, m)}
    sent = range(outside if last else BLOCKS)
    relayed = len(sent) // 2
    sides, bands, edges = {}, {}, {}
    for q in range(BLOCKS):
        for h in (-1, 1):
            for d in (-1, 1):
                sides[h, q, d] = Side(
                    around, "cols", d, grad_ref.at[:, lines[h, q], cut[d]], side_ref.at[(d + 1) // 2, :, lines[h, q]]
                )
                if not last:
                    edges[h, q, d] = Side(
                        around, "cols", d, out_ref.at[:, lines[h, q], inner[d]], out_ref.at[:, lines[h, q], cut[-d]]
                    )
            if q not in sent:
                continue
            source, target = mid_ref.at[:, lines[h, q]], band_ref.at[:, lines[-h, BLOCKS - 1 - q]]
            if around.relays and q < relayed:
                bands[h, q] = Hop(around, h, source, target, relay_ref.at[q, :, pl.ds(0, part)])
            else:
                bands[h, q] = Side(around, "rows", h, source, target)
    for side in sides.values():
        side.start()
    if not last:
        for d in (-1, 1):

            @pl.when(no(here["cols", d]))
            def _():
                out_ref[:, :, cut[d]] = jnp.zeros((planes, extent, m), jnp.float32)

    def gather(h, q):
        mid_ref[:, lines[h, q]] = grad_ref[:, lines[h, q], m : m + wide]
        for d in (-1, 1):
            target = pl.ds(0, m) if d < 0 else pl.ds(wide - m, m)

            @pl.when(here["cols", d])
            def _():
                sides[h, q, -d].straight.wait_recv()
                mid_ref[:, lines[h, q], target] += side_ref[(1 - d) // 2, :, lines[h, q]]

    def finish(h, q):
        rows = lines[h, q]
        place = (slice(None), pl.ds(rows.start - m, part)) if last else (slice(None), rows, slice(m, m + wide))

        @pl.when(here["rows", h])
        def _():
            bands[-h, BLOCKS - 1 - q].straight.wait_recv()
            total = mid_ref[:, rows] + band_ref[:, rows]
            out_ref[place] = padded_ref[:, rows, m : m + wide] - step_rate * total

        @pl.when(no(here["rows", h]))
        def _():
            if q < outside:
                out_ref[place] = jnp.zeros((planes, part, wide), jnp.float32)
            else:
                out_ref[place] = padded_ref[:, rows, m : m + wide] - step_rate * mid_ref[:, rows]

        if not last:
            for d in (-1, 1):
                edges[h, q, d].start()

    def by_parity(work):
        for far in (-1, 1):
            pl.when(around.far[far])(functools.partial(work, far))

    for q in range(BLOCKS):
        for h in (-1, 1):
            gather(h, q)
            if q in sent:
                bands[h, q].start()
    for band in bands.values():
        band.forward()

    def finish_all(far):
        near = [(-far, q) for q in sent]
        order = near[:relayed]
        for q in sent[relayed:]:
            order += [near[q], (far, q)]
        for h, q in order + [(far, q) for q in sent[:relayed]]:
            finish(h, BLOCKS - 1 - q)

    by_parity(finish_all)
    for edge in edges.values():
        edge.wait_recv()
    def rest():
        for copy in [*bands.values(), *edges.values(), *sides.values()]:
            copy.wait_left()
            copy.wait_forwarded()

    return rest


def whole_kernel(
    positions_ref,
    field_ref,
    intensity_ref,
    probes_ref,
    table_from,
    out_ref,
    *refs,
):
    padded_refs, refs = refs[:ITERS], refs[ITERS:]
    work(
        positions_ref, field_ref, intensity_ref, probes_ref, table_from, out_ref, padded_refs, *refs
    )


def work(
    positions_ref,
    field_ref,
    intensity_ref,
    probes_ref,
    table_from,
    out_ref,
    padded_refs,
    grad_ref,
    measured_ref,
    raw_ref,
    table_ref,
    mid_ref,
    side_ref,
    band_ref,
    relay_ref,
    send_sems,
    recv_sems,
    local_sems,
):
    m = MARGIN
    planes, high, wide = field_ref.shape
    slots, size, _ = measured_ref.shape
    parts = size // LANES
    own = pltpu.make_async_copy(
        field_ref, padded_refs[0].at[:, pl.ds(m, high), pl.ds(m, wide)], local_sems.at[slots * parts]
    )
    fetches = [
        pltpu.make_async_copy(
            intensity_ref.at[0, 0, k, :, pl.ds(c * LANES, LANES)], raw_ref.at[k, c], local_sems.at[k * parts + c]
        )
        for k in range(slots)
        for c in range(parts)
    ]
    held = pltpu.make_async_copy(table_from, table_ref, local_sems.at[slots * parts + 1])
    for copy in [own, *fetches, held]:
        copy.start()
    around = Around(send_sems, recv_sems)
    around.meet()

    def meanwhile():
        grad_ref[...] = jnp.zeros_like(grad_ref)
        order = order_columns(size)
        for k in range(slots):
            for c in range(parts):
                fetches[k * parts + c].wait()
            put_in_order(raw_ref.at[k], measured_ref.at[k], order)
        for copy in [own, held]:
            copy.wait()

    rests = [pad(around, field_ref, padded_refs[0], relay_ref.at[0], meanwhile)]
    for k in range(ITERS):
        last = k == ITERS - 1
        add_terms(
            positions_ref, padded_refs[k], probes_ref, measured_ref, table_ref, grad_ref.at[k]
        )
        target = out_ref if last else padded_refs[k + 1]
        scratch = [ref.at[k] for ref in (mid_ref, side_ref, band_ref)]
        rests.append(step(last, around, grad_ref.at[k], padded_refs[k], target, *scratch, relay_ref.at[k + 1]))
    for rest in rests:
        rest()


def on_device(object_field, probe, positions, counts, intensity):
    planes, high, wide = object_field.shape
    slots, size, _ = intensity.shape[2:]
    table = jnp.asarray(tables(size))
    tall, broad = high + 2 * MARGIN, wide + 2 * MARGIN
    assert tall == broad == 2 * size
    copies = 64 * (ITERS + 1)
    floats = [
        *[(planes, tall, broad)] * ITERS,
        (ITERS, planes, tall, broad),
        (slots, size, size),
    ]
    blocks = [
        (ITERS, planes, tall, wide),
        (ITERS, 2, planes, tall, MARGIN),
        (ITERS, planes, tall, wide),
        (ITERS + 1, BLOCKS // 2, planes, MARGIN, wide),
    ]
    positions = positions[0, 0].T
    probes = pl.pallas_call(
        turn_kernel,
        out_shape=jax.ShapeDtypeStruct((slots, *probe.shape), jnp.float32),
        in_specs=[pl.BlockSpec(memory_space=pltpu.SMEM)] * 2 + [pl.BlockSpec(memory_space=pltpu.VMEM)],
        out_specs=pl.BlockSpec(memory_space=pltpu.VMEM),
        scratch_shapes=[pltpu.VMEM((planes, 2 * size, size), jnp.float32)],
        compiler_params=pltpu.CompilerParams(vmem_limit_bytes=12 * 1024 * 1024),
        name="turn",
    )(positions, counts, probe)
    held = [pltpu.with_memory_space_constraint(array, pltpu.HBM) for array in (object_field, intensity, table)]
    return pl.pallas_call(
        whole_kernel,
        out_shape=jax.ShapeDtypeStruct(object_field.shape, jnp.float32),
        in_specs=[pl.BlockSpec(memory_space=pltpu.SMEM)]
        + [pl.BlockSpec(memory_space=pltpu.HBM)] * 2
        + [pl.BlockSpec(memory_space=pltpu.VMEM), pl.BlockSpec(memory_space=pltpu.HBM)],
        out_specs=pl.BlockSpec(memory_space=pltpu.VMEM),
        scratch_shapes=[pltpu.VMEM(shape, jnp.float32) for shape in floats]
        + [
            pltpu.VMEM((slots, size // LANES, size, LANES), jnp.int32),
            pltpu.VMEM(table.shape, jnp.bfloat16),
        ]
        + [pltpu.VMEM(shape, jnp.float32) for shape in blocks]
        + [
            pltpu.SemaphoreType.DMA((copies,)),
            pltpu.SemaphoreType.DMA((copies,)),
            pltpu.SemaphoreType.DMA((slots * (size // LANES) + 3,)),
        ],
        compiler_params=pltpu.CompilerParams(
            collective_id=0, has_side_effects=True, vmem_limit_bytes=48 * 1024 * 1024
        ),
        name="whole",
    )(positions, *held[:2], probes, held[2])


def solution(mesh):
    placed = (
        P(None, "rows", "cols"),
        P(),
        P("rows", "cols", None, None),
        P("rows", "cols"),
        P("rows", "cols", None, None, None),
    )
    return jax.shard_map(
        on_device, mesh=mesh, in_specs=placed, out_specs=P(None, "rows", "cols"), check_vma=False
    )
```

time: 81 us -> 81.3 us (level); the launches traced: 81 us -> 80.2 us
  Pallas kernels: 79.3 us -> 77 us
  local copies, waits for them, and re-layouts: 0.81 us -> 2.51 us
    pallas_call x5 -> x2, Pallas kernels: 79.3 us -> 77 us  [the longest x1 75.8 us: on_device(): pl.pallas_call(whole_kernel, out_shape=jax.ShapeDtypeStruct(object_field....]
    unnamed x7, local copies, waits for them, and re-layouts: 0.81 us -> 2.51 us
where the time goes in v3:
time: 81.3 us; the launch traced here: 80.2 us
  Pallas kernels  77 us (95%)
  local copies, waits for them, and re-layouts  2.51 us (3%)
    pallas_call x1, Pallas kernels, on_device(): pl.pallas_call(whole_kernel, out_shape=jax.ShapeDtypeStruct(object_field....  75.8 us
    unnamed x7, local copies, waits for them, and re-layouts  2.51 us

profile of v3, /device:TPU:5, one launch (start us, length us, event | category | flops | bytes accessed | tf_op | source)
XLA Modules:
  0.0 80.2 jit_solution(13587353627260245985)
XLA Ops:
  0.0 0.0 copy-start.2
  0.7 0.0 copy-start
  0.7 1.0 %copy-done = f32[2,256,256]{2,1,0:T(8,128)S(1)} copy-done((f32[2,256,256]{2,1,0:T(8,128)S(1)}, f32[2,256,256]{2,1,0:T(8,128)}, u32[]{:S(2)}) %copy-start) | copy-done | bytes 524312
  1.7 0.0 copy-start.1
  1.7 0.7 copy-done.1
  2.4 1.2 %turn.1.probes_ref = f32[6,2,256,256]{3,2,1,0:T(8,128)S(1)} custom-call(s32[2,6]{1,0:T(2,128)S(1)} %bitcast.3, s32[1,1]{1,0:T(1,128)S(6)} %copy.8.counts_ref, f32[2,256,256]{2,1,0:T(8,128)S(1)} %copy-done), custom_call_target="tpu_custom_call" | custom-call | tf_op jit(solution)/shard_map/turn/pallas_call | solution.py:595
  3.6 0.0 copy-done.2
  3.6 75.8 %whole.1 = f32[2,256,256]{2,1,0:T(8,128)S(1)} custom-call(s32[2,6]{1,0:T(2,128)S(1)} %bitcast.4, f32[2,256,256]{2,1,0:T(8,128)} %field_ref.1, s32[1,1,6,256,256]{4,3,2,1,0:T(8,128)} %intensity_ref.1, f32[6,2,256,256]{3,2,1,0:T(8,128)S(1)} %turn.1.probes_ref, bf16[2,4,256,256]{3,2,1,0:T(8,128)(2,1)} %constant.2.clone.table_from), custom_call_target="tpu_custom_call" | custom-call | tf_op jit(solution)/shard_map/whole/pallas_call | solution.py:605
  79.4 0.8 copy.9
Async XLA Ops:
  0.0 3.6 %copy-start.2 = (s32[1,1,6,2]{2,3,1,0:T(2,128)S(1)}, s32[1,1,6,2]{2,3,1,0:T(2,128)}, u32[]{:S(2)}) copy-start(s32[1,1,6,2]{2,3,1,0:T(2,128)} %param.8) | copy-start | bytes 148
  0.7 1.0 %copy-start = (f32[2,256,256]{2,1,0:T(8,128)S(1)}, f32[2,256,256]{2,1,0:T(8,128)}, u32[]{:S(2)}) copy-start(f32[2,256,256]{2,1,0:T(8,128)} %probe_ref.1) | copy-start | bytes 1572868
  1.7 0.7 copy-start.1

commit v4 on v3

--- a/solution.py
+++ b/solution.py
@@ -85,11 +85,11 @@
 
 def turned(value, drop, shift):
     rows, columns = value.shape
-    groups = pltpu.roll(value.reshape(rows // ROWS, ROWS, columns), drop % ROWS, 1)
+    groups = pltpu.roll(value.reshape(rows // ROWS, ROWS, columns), drop, 1)
     before = jnp.concatenate([groups[-1:], groups[:-1]], axis=0)
     within = lax.broadcasted_iota(jnp.int32, (1, ROWS, columns), 1) >= drop
     value = jnp.where(within, groups, before).reshape(rows, columns)
-    parts = [pltpu.roll(value[:, c : c + LANES], shift % LANES, 1) for c in range(0, columns, LANES)]
+    parts = [pltpu.roll(value[:, c : c + LANES], shift, 1) for c in range(0, columns, LANES)]
     within = lax.broadcasted_iota(jnp.int32, (rows, LANES), 1) >= shift
     return jnp.concatenate([jnp.where(within, a, b) for a, b in zip(parts, parts[-1:] + parts[:-1])], axis=1)
 
@@ -158,30 +158,25 @@
         works = [work for work in works if next(work, works) is not works]
 
 
-def turn_kernel(positions_ref, counts_ref, probe_ref, probes_ref, twice_ref):
-    planes, size, _ = probe_ref.shape
-    slots = probes_ref.shape[0]
-    count = counts_ref[0, 0]
-
-    @pl.loop(0, count)
-    def _(slot):
-        row = lax.rem(positions_ref[0, slot], size)
-        column = lax.rem(positions_ref[1, slot], size)
-        drop, shift = lax.rem(row, ROWS), lax.rem(column, LANES)
-        first = pl.multiple_of(size - (row - drop), ROWS)
-        for p in range(planes):
-            value = turned(probe_ref[p], drop, shift)
-            parts = [value[:, c : c + LANES] for c in range(0, size, LANES)]
-            for k in range(1, size // LANES):
-                moved = jnp.concatenate(parts[-k:] + parts[:-k], axis=1)
-                value = jnp.where(column // LANES == k, moved, value)
-            twice_ref[p, :size] = value
-            twice_ref[p, size:] = value
-            probes_ref[slot, p] = twice_ref[p, pl.ds(first, size)]
-
-    @pl.loop(count, slots)
-    def _(slot):
-        probes_ref[slot] = jnp.zeros(probes_ref.shape[1:], jnp.float32)
+def roll_probe(live, row, column, probe):
+    rows, columns = probe.shape
+    each = lax.broadcasted_iota(jnp.int32, probe.shape, 1)
+
+    def picked(flag, first, second):
+        return jnp.where(each < flag * columns, first, second)
+
+    value = turned(probe, lax.rem(row, ROWS), lax.rem(column, LANES))
+    step = LANES
+    while step < columns:
+        moved = jnp.concatenate([value[:, columns - step :], value[:, : columns - step]], axis=1)
+        value = picked(lax.rem(lax.div(column, step), 2), moved, value)
+        step *= 2
+    step = ROWS
+    while step < rows:
+        moved = jnp.concatenate([value[rows - step :], value[: rows - step]], axis=0)
+        value = picked(lax.rem(lax.div(row, step), 2), moved, value)
+        step *= 2
+    return picked(live, value, 0.0)
 
 
 def add_terms(positions_ref, padded_ref, probes_ref, measured_ref, table_ref, grad_ref):
@@ -317,7 +312,7 @@
     return jnp.logical_not(flag)
 
 
-def pad(around, field_ref, out_ref, relay_ref, meanwhile):
+def pad(around, field_ref, out_ref, relay_ref, meanwhile, afterwards):
     m = MARGIN
     planes, high, wide = field_ref.shape
     here = around.here
@@ -369,6 +364,7 @@
     meanwhile()
     for d in (-1, 1):
         rows[d, 0].forward()
+    afterwards()
     for far in (-1, 1):
 
         @pl.when(around.far[far])
@@ -497,30 +493,34 @@
 
 def whole_kernel(
     positions_ref,
+    counts_ref,
     field_ref,
     intensity_ref,
-    probes_ref,
+    probe_from,
     table_from,
     out_ref,
     *refs,
 ):
     padded_refs, refs = refs[:ITERS], refs[ITERS:]
     work(
-        positions_ref, field_ref, intensity_ref, probes_ref, table_from, out_ref, padded_refs, *refs
+        positions_ref, counts_ref, field_ref, intensity_ref, probe_from, table_from, out_ref, padded_refs, *refs
     )
 
 
 def work(
     positions_ref,
+    counts_ref,
     field_ref,
     intensity_ref,
-    probes_ref,
+    probe_from,
     table_from,
     out_ref,
     padded_refs,
     grad_ref,
     measured_ref,
+    probes_ref,
     raw_ref,
+    probe_ref,
     table_ref,
     mid_ref,
     side_ref,
@@ -544,8 +544,11 @@
         for k in range(slots)
         for c in range(parts)
     ]
-    held = pltpu.make_async_copy(table_from, table_ref, local_sems.at[slots * parts + 1])
-    for copy in [own, *fetches, held]:
+    held = [
+        pltpu.make_async_copy(source, target, local_sems.at[slots * parts + 1 + k])
+        for k, (source, target) in enumerate([(probe_from, probe_ref), (table_from, table_ref)])
+    ]
+    for copy in [own, *fetches, *held]:
         copy.start()
     around = Around(send_sems, recv_sems)
     around.meet()
@@ -557,10 +560,18 @@
             for c in range(parts):
                 fetches[k * parts + c].wait()
             put_in_order(raw_ref.at[k], measured_ref.at[k], order)
-        for copy in [own, held]:
+
+    def afterwards():
+        for copy in [own, *held]:
             copy.wait()
 
-    rests = [pad(around, field_ref, padded_refs[0], relay_ref.at[0], meanwhile)]
+        @pl.loop(0, slots)
+        def _(slot):
+            live = counts_ref[0, 0] - slot
+            for p in range(planes):
+                probes_ref[slot, p] = roll_probe(live, positions_ref[0, slot], positions_ref[1, slot], probe_ref[p])
+
+    rests = [pad(around, field_ref, padded_refs[0], relay_ref.at[0], meanwhile, afterwards)]
     for k in range(ITERS):
         last = k == ITERS - 1
         add_terms(
@@ -584,6 +595,7 @@
         *[(planes, tall, broad)] * ITERS,
         (ITERS, planes, tall, broad),
         (slots, size, size),
+        (slots, planes, size, size),
     ]
     blocks = [
         (ITERS, planes, tall, wide),
@@ -591,27 +603,16 @@
         (ITERS, planes, tall, wide),
         (ITERS + 1, BLOCKS // 2, planes, MARGIN, wide),
     ]
-    positions = positions[0, 0].T
-    probes = pl.pallas_call(
-        turn_kernel,
-        out_shape=jax.ShapeDtypeStruct((slots, *probe.shape), jnp.float32),
-        in_specs=[pl.BlockSpec(memory_space=pltpu.SMEM)] * 2 + [pl.BlockSpec(memory_space=pltpu.VMEM)],
-        out_specs=pl.BlockSpec(memory_space=pltpu.VMEM),
-        scratch_shapes=[pltpu.VMEM((planes, 2 * size, size), jnp.float32)],
-        compiler_params=pltpu.CompilerParams(vmem_limit_bytes=12 * 1024 * 1024),
-        name="turn",
-    )(positions, counts, probe)
-    held = [pltpu.with_memory_space_constraint(array, pltpu.HBM) for array in (object_field, intensity, table)]
+    held = [pltpu.with_memory_space_constraint(array, pltpu.HBM) for array in (object_field, intensity, probe, table)]
     return pl.pallas_call(
         whole_kernel,
         out_shape=jax.ShapeDtypeStruct(object_field.shape, jnp.float32),
-        in_specs=[pl.BlockSpec(memory_space=pltpu.SMEM)]
-        + [pl.BlockSpec(memory_space=pltpu.HBM)] * 2
-        + [pl.BlockSpec(memory_space=pltpu.VMEM), pl.BlockSpec(memory_space=pltpu.HBM)],
+        in_specs=[pl.BlockSpec(memory_space=pltpu.SMEM)] * 2 + [pl.BlockSpec(memory_space=pltpu.HBM)] * len(held),
         out_specs=pl.BlockSpec(memory_space=pltpu.VMEM),
         scratch_shapes=[pltpu.VMEM(shape, jnp.float32) for shape in floats]
         + [
             pltpu.VMEM((slots, size // LANES, size, LANES), jnp.int32),
+            pltpu.VMEM(probe.shape, jnp.float32),
             pltpu.VMEM(table.shape, jnp.bfloat16),
         ]
         + [pltpu.VMEM(shape, jnp.float32) for shape in blocks]
@@ -624,7 +625,7 @@
             collective_id=0, has_side_effects=True, vmem_limit_bytes=48 * 1024 * 1024
         ),
         name="whole",
-    )(positions, *held[:2], probes, held[2])
+    )(positions[0, 0].T, counts, *held)
 
 
 def solution(mesh):

time: 81.3 us -> 77.9 us (0.958)
  Pallas kernels: 77 us -> 74.8 us
  local copies, waits for them, and re-layouts: 2.51 us -> 1.47 us
    pallas_call x1 -> x0, Pallas kernels: 1.16 us -> none  [on_device(): pl.pallas_call(turn_kernel, out_shape=jax.ShapeDtypeStruct((slots, *probe...]
    unnamed x7 -> x3, local copies, waits for them, and re-layouts: 2.51 us -> 1.47 us
    pallas_call x1, Pallas kernels: 75.8 us -> 74.8 us  [on_device(): pl.pallas_call(whole_kernel, out_shape=jax.ShapeDtypeStruct(object_field....]
where the time goes in v4:
time: 77.9 us; the launch traced here: 77 us
  Pallas kernels  74.8 us (96%)
  local copies, waits for them, and re-layouts  1.47 us (2%)
    pallas_call x1, Pallas kernels, on_device(): pl.pallas_call(whole_kernel, out_shape=jax.ShapeDtypeStruct(object_field....  74.8 us

profile of v4, /device:TPU:5, one launch (start us, length us, event | category | flops | bytes accessed | tf_op | source)
XLA Modules:
  0.0 77.0 jit_solution(17219615301044273856)
XLA Ops:
  0.7 0.0 copy-start
  0.7 0.7 copy-done
  1.3 74.8 %whole.1 = f32[2,256,256]{2,1,0:T(8,128)S(1)} custom-call(s32[2,6]{1,0:T(2,128)S(1)} %bitcast.3, s32[1,1]{1,0:T(1,128)S(6)} %copy.8.counts_ref, f32[2,256,256]{2,1,0:T(8,128)} %field_ref.1, s32[1,1,6,256,256]{4,3,2,1,0:T(8,128)} %intensity_ref.1, f32[2,256,256]{2,1,0:T(8,128)} %probe_from.1, bf16[2,4,256,256]{3,2,1,0:T(8,128)(2,1)} %constant.2.clone.table_from), custom_call_target="tpu_custom_call" | custom-call | tf_op jit(solution)/shard_map/whole/pallas_call | solution.py:607
  76.2 0.8 %copy.9 = f32[2,256,256]{2,1,0:T(8,128)} copy(f32[2,256,256]{2,1,0:T(8,128)S(1)} %whole.1) | data formatting | bytes 1048576
Async XLA Ops:
  0.7 0.7 copy-start

commit v5 on v4

--- a/solution.py
+++ b/solution.py
@@ -14,7 +14,7 @@
 LANES = 128
 ROWS = 8
 PAIR = 2
-BLOCKS = 4
+BLOCKS = 2
 
 
 step_rate = 0.02
@@ -219,6 +219,8 @@
         self.relays = count > 2 and count % 2 == 0
         odd = lax.rem(lax.axis_index("rows"), 2) == 1
         self.far = {1: odd, -1: no(odd)}
+        even = lax.rem(lax.axis_index("cols"), 2) == 0
+        self.quick = {1: even, -1: no(even)}
 
     def meet(self):
         barrier = pltpu.get_barrier_semaphore()
@@ -272,14 +274,15 @@
 
 
 class Hop:
-    def __init__(self, around, d, source, target, relay):
-        here, far = around.here["rows", d], around.far[d]
+    def __init__(self, around, d, c, source, target, relay):
+        here = around.here["rows", d]
+        by = both(around.far[d], around.quick[c]) if around.relays else False
         self.back = around.here["rows", -d]
         recv = around.new_recv()
         self.straight = around.copy(("rows", d), source, target, recv)
-        self.near = both(here, no(far))
-        self.long = both(here, far)
-        self.middle = both(around.here["rows", -2 * d], far)
+        self.near = both(here, no(by))
+        self.long = both(here, by)
+        self.middle = both(around.here["rows", -2 * d], by)
         self.first = around.copy(("rows", 2 * d), source, relay)
         self.second = around.copy(("rows", -d), relay, target, recv)
 
@@ -316,30 +319,35 @@
     m = MARGIN
     planes, high, wide = field_ref.shape
     here = around.here
-    part = m // 2
-    row_from = {(-1, q): pl.ds(q * part, part) for q in (0, 1)} | {(1, q): pl.ds(high - m + q * part, part) for q in (0, 1)}
-    row_land = {(1, q): pl.ds(q * part, part) for q in (0, 1)} | {(-1, q): pl.ds(m + high + q * part, part) for q in (0, 1)}
+    sides = (-1, 1)
+    row_from = {-1: pl.ds(0, m), 1: pl.ds(high - m, m)}
+    row_land = {1: pl.ds(0, m), -1: pl.ds(m + high, m)}
+    half = {-1: pl.ds(0, m), 1: pl.ds(wide - m, m)}
+    inner = {-1: pl.ds(m, m), 1: pl.ds(wide, m)}
     col_cuts = {-1: (pl.ds(0, m), pl.ds(m + wide, m)), 1: (pl.ds(wide - m, m), pl.ds(0, m))}
     from_cuts = {-1: pl.ds(0, m), 1: pl.ds(m + high, m)}
-    col_from = {-1: pl.ds(m, m), 1: pl.ds(wide, m)}
     rows, cols, corners = {}, {}, {}
-    for d in (-1, 1):
-        for q in (0, 1):
-            source, target = field_ref.at[:, row_from[d, q]], out_ref.at[:, row_land[d, q], pl.ds(m, wide)]
-            if around.relays and q == 0:
-                rows[d, q] = Hop(around, d, source, target, relay_ref.at[0, :, pl.ds(0, part)])
-            else:
-                rows[d, q] = Side(around, "rows", d, source, target)
+    for d in sides:
         cut, land = col_cuts[d]
         cols[d] = Side(around, "cols", d, field_ref.at[:, :, cut], out_ref.at[:, pl.ds(m, high), land])
-        for v in (-1, 1):
-            for q in (0, 1):
-                lines = row_land[-v, q]
-                corners[v, q, d] = around.copy(("cols", d), out_ref.at[:, lines, col_from[d]], out_ref.at[:, lines, land])
-    for q in (0, 1):
-        for d in (-1, 1):
-            rows[d, q].start()
-    for d in (-1, 1):
+        for c in sides:
+            source, target = field_ref.at[:, row_from[d], half[c]], out_ref.at[:, row_land[d], inner[c]]
+            rows[d, c] = Hop(around, d, c, source, target, relay_ref.at[0, :, pl.ds(0, m), pl.ds(0, m)])
+            corners[d, c] = around.copy(
+                ("cols", c), out_ref.at[:, from_cuts[d], inner[c]], out_ref.at[:, from_cuts[d], col_cuts[c][1]]
+            )
+
+    def slow_first(work):
+        for c in sides:
+            pl.when(around.quick[-c])(functools.partial(work, (c, -c)))
+
+    @slow_first
+    def _(order):
+        for c in order:
+            for d in sides:
+                rows[d, c].start()
+
+    for d in sides:
         cols[d].start()
     for v in (-1, 1):
 
@@ -362,29 +370,29 @@
             out_ref[:, m : m + high, land] = jnp.zeros((planes, high, m), jnp.float32)
 
     meanwhile()
-    for d in (-1, 1):
-        rows[d, 0].forward()
+    for hop in rows.values():
+        hop.forward()
     afterwards()
-    for far in (-1, 1):
-
-        @pl.when(around.far[far])
-        def _():
-            for v, q in ((-far, 0), (-far, 1), (far, 1), (far, 0)):
-                rows[-v, q].wait_recv()
-                for d in (-1, 1):
-                    pl.when(both(here["rows", v], here["cols", d]))(corners[v, q, d].start)
-
-    for d in (-1, 1):
+
+    def receive(far, order):
+        for c in order:
+            for v in (-far, far):
+                rows[-v, c].wait_recv()
+                pl.when(both(here["rows", v], here["cols", c]))(corners[v, c].start)
+
+    for far in sides:
+        pl.when(around.far[far])(lambda far=far: slow_first(functools.partial(receive, far)))
+    for d in sides:
         cols[-d].wait_recv()
-        for v in (-1, 1):
-            for q in (0, 1):
-                pl.when(both(here["rows", v], here["cols", d]))(corners[v, q, -d].wait_recv)
+        for v in sides:
+            pl.when(both(here["rows", v], here["cols", d]))(corners[v, -d].wait_recv)
+
     def rest():
         for copy in [*rows.values(), *cols.values()]:
             copy.wait_left()
             copy.wait_forwarded()
-        for v, q, d in corners:
-            pl.when(both(here["rows", v], here["cols", d]))(corners[v, q, d].wait_send)
+        for v, c in corners:
+            pl.when(both(here["rows", v], here["cols", c]))(corners[v, c].wait_send)
 
     return rest
 
@@ -396,30 +404,23 @@
     part = extent // 2 // BLOCKS
     outside = m // part
     here = around.here
-    begin = {(h, q): q * part if h < 0 else extent - (q + 1) * part for h in (-1, 1) for q in range(BLOCKS)}
+    begin = {(h, q): q * part if h < 0 else extent - (q + 1) * part for q in range(BLOCKS) for h in (-1, 1)}
     lines = {key: pl.ds(start, part) for key, start in begin.items()}
     cut = {-1: pl.ds(0, m), 1: pl.ds(extent - m, m)}
     inner = {-1: pl.ds(m, m), 1: pl.ds(wide, m)}
+    half = {-1: pl.ds(0, m), 1: pl.ds(wide - m, m)}
     sent = range(outside if last else BLOCKS)
-    relayed = len(sent) // 2
     sides, bands, edges = {}, {}, {}
-    for q in range(BLOCKS):
-        for h in (-1, 1):
-            for d in (-1, 1):
-                sides[h, q, d] = Side(
-                    around, "cols", d, grad_ref.at[:, lines[h, q], cut[d]], side_ref.at[(d + 1) // 2, :, lines[h, q]]
-                )
-                if not last:
-                    edges[h, q, d] = Side(
-                        around, "cols", d, out_ref.at[:, lines[h, q], inner[d]], out_ref.at[:, lines[h, q], cut[-d]]
-                    )
-            if q not in sent:
-                continue
-            source, target = mid_ref.at[:, lines[h, q]], band_ref.at[:, lines[-h, BLOCKS - 1 - q]]
-            if around.relays and q < relayed:
-                bands[h, q] = Hop(around, h, source, target, relay_ref.at[q, :, pl.ds(0, part)])
-            else:
-                bands[h, q] = Side(around, "rows", h, source, target)
+    for h, q in lines:
+        for d in (-1, 1):
+            rows = lines[h, q]
+            sides[h, q, d] = Side(around, "cols", d, grad_ref.at[:, rows, cut[d]], side_ref.at[(d + 1) // 2, :, rows])
+            if not last:
+                edges[h, q, d] = Side(around, "cols", d, out_ref.at[:, rows, inner[d]], out_ref.at[:, rows, cut[-d]])
+            if q in sent:
+                source, target = mid_ref.at[:, rows, half[d]], band_ref.at[:, lines[-h, BLOCKS - 1 - q], half[d]]
+                relay = relay_ref.at[q, :, pl.ds(0, part), pl.ds(0, m)]
+                bands[h, q, d] = Hop(around, h, d, source, target, relay)
     for side in sides.values():
         side.start()
     if not last:
@@ -429,58 +430,57 @@
             def _():
                 out_ref[:, :, cut[d]] = jnp.zeros((planes, extent, m), jnp.float32)
 
-    def gather(h, q):
-        mid_ref[:, lines[h, q]] = grad_ref[:, lines[h, q], m : m + wide]
-        for d in (-1, 1):
-            target = pl.ds(0, m) if d < 0 else pl.ds(wide - m, m)
-
-            @pl.when(here["cols", d])
-            def _():
-                sides[h, q, -d].straight.wait_recv()
-                mid_ref[:, lines[h, q], target] += side_ref[(1 - d) // 2, :, lines[h, q]]
-
-    def finish(h, q):
+    def gather(h, q, d):
         rows = lines[h, q]
-        place = (slice(None), pl.ds(rows.start - m, part)) if last else (slice(None), rows, slice(m, m + wide))
+        mid_ref[:, rows, half[d]] = grad_ref[:, rows, inner[d]]
+
+        @pl.when(here["cols", d])
+        def _():
+            sides[h, q, -d].straight.wait_recv()
+            mid_ref[:, rows, half[d]] += side_ref[(1 - d) // 2, :, rows]
+
+    def finish(h, q, d):
+        rows = lines[h, q]
+        place = (slice(None), pl.ds(rows.start - m, part), half[d]) if last else (slice(None), rows, inner[d])
 
         @pl.when(here["rows", h])
         def _():
-            bands[-h, BLOCKS - 1 - q].straight.wait_recv()
-            total = mid_ref[:, rows] + band_ref[:, rows]
-            out_ref[place] = padded_ref[:, rows, m : m + wide] - step_rate * total
+            bands[-h, BLOCKS - 1 - q, d].straight.wait_recv()
+            total = mid_ref[:, rows, half[d]] + band_ref[:, rows, half[d]]
+            out_ref[place] = padded_ref[:, rows, inner[d]] - step_rate * total
 
         @pl.when(no(here["rows", h]))
         def _():
             if q < outside:
-                out_ref[place] = jnp.zeros((planes, part, wide), jnp.float32)
+                out_ref[place] = jnp.zeros((planes, part, m), jnp.float32)
             else:
-                out_ref[place] = padded_ref[:, rows, m : m + wide] - step_rate * mid_ref[:, rows]
+                out_ref[place] = padded_ref[:, rows, inner[d]] - step_rate * mid_ref[:, rows, half[d]]
 
         if not last:
-            for d in (-1, 1):
-                edges[h, q, d].start()
-
-    def by_parity(work):
-        for far in (-1, 1):
-            pl.when(around.far[far])(functools.partial(work, far))
-
-    for q in range(BLOCKS):
-        for h in (-1, 1):
-            gather(h, q)
-            if q in sent:
-                bands[h, q].start()
+            edges[h, q, d].start()
+
+    def begin_all(quick):
+        for d in (quick, -quick):
+            for q in range(BLOCKS):
+                for h in (-1, 1):
+                    gather(h, q, d)
+                    if q in sent:
+                        bands[h, q, d].start()
+
+    def finish_all(far, quick):
+        order = [(-far, q, quick) for q in sent]
+        for q in sent:
+            order += [(far, q, -quick), (-far, q, -quick)]
+        for h, q, d in order + [(far, q, quick) for q in sent]:
+            finish(h, BLOCKS - 1 - q, d)
+
+    for quick in (-1, 1):
+        pl.when(around.quick[quick])(functools.partial(begin_all, quick))
     for band in bands.values():
         band.forward()
-
-    def finish_all(far):
-        near = [(-far, q) for q in sent]
-        order = near[:relayed]
-        for q in sent[relayed:]:
-            order += [near[q], (far, q)]
-        for h, q in order + [(far, q) for q in sent[:relayed]]:
-            finish(h, BLOCKS - 1 - q)
-
-    by_parity(finish_all)
+    for far in (-1, 1):
+        for quick in (-1, 1):
+            pl.when(both(around.far[far], around.quick[quick]))(functools.partial(finish_all, far, quick))
     for edge in edges.values():
         edge.wait_recv()
     def rest():
@@ -589,7 +589,7 @@
     slots, size, _ = intensity.shape[2:]
     table = jnp.asarray(tables(size))
     tall, broad = high + 2 * MARGIN, wide + 2 * MARGIN
-    assert tall == broad == 2 * size
+    assert tall == broad == 2 * size and wide == 2 * MARGIN
     copies = 64 * (ITERS + 1)
     floats = [
         *[(planes, tall, broad)] * ITERS,
@@ -601,7 +601,7 @@
         (ITERS, planes, tall, wide),
         (ITERS, 2, planes, tall, MARGIN),
         (ITERS, planes, tall, wide),
-        (ITERS + 1, BLOCKS // 2, planes, MARGIN, wide),
+        (ITERS + 1, BLOCKS, planes, MARGIN, MARGIN),
     ]
     held = [pltpu.with_memory_space_constraint(array, pltpu.HBM) for array in (object_field, intensity, probe, table)]
     return pl.pallas_call(

time: 77.9 us -> 71.1 us (0.913)
  Pallas kernels: 74.8 us -> 67.7 us
    pallas_call x1, Pallas kernels: 74.8 us -> 67.7 us  [on_device(): pl.pallas_call(whole_kernel, out_shape=jax.ShapeDtypeStruct(object_field....]
where the time goes in v5:
time: 71.1 us; the launch traced here: 69.9 us
  Pallas kernels  67.7 us (95%)
  local copies, waits for them, and re-layouts  1.47 us (2%)
    pallas_call x1, Pallas kernels, on_device(): pl.pallas_call(whole_kernel, out_shape=jax.ShapeDtypeStruct(object_field....  67.7 us
    unnamed x3, local copies, waits for them, and re-layouts  1.47 us

profile of v5, /device:TPU:5, one launch (start us, length us, event | category | flops | bytes accessed | tf_op | source)
XLA Modules:
  0.0 69.9 jit_solution(9604551333136943900)
XLA Ops:
  0.7 0.0 copy-start
  0.7 0.7 copy-done
  1.3 67.7 %whole.1 = f32[2,256,256]{2,1,0:T(8,128)S(1)} custom-call(s32[2,6]{1,0:T(2,128)S(1)} %bitcast.3, s32[1,1]{1,0:T(1,128)S(6)} %copy.8.counts_ref, f32[2,256,256]{2,1,0:T(8,128)} %field_ref.1, s32[1,1,6,256,256]{4,3,2,1,0:T(8,128)} %intensity_ref.1, f32[2,256,256]{2,1,0:T(8,128)} %probe_from.1, bf16[2,4,256,256]{3,2,1,0:T(8,128)(2,1)} %constant.2.clone.table_from), custom_call_target="tpu_custom_call" | custom-call | tf_op jit(solution)/shard_map/whole/pallas_call | solution.py:607
  69.1 0.8 %copy.9 = f32[2,256,256]{2,1,0:T(8,128)} copy(f32[2,256,256]{2,1,0:T(8,128)S(1)} %whole.1) | data formatting | bytes 1048576
Async XLA Ops:
  0.7 0.7 copy-start

commit v6 on v5

--- a/solution.py
+++ b/solution.py
@@ -222,7 +222,7 @@
         even = lax.rem(lax.axis_index("cols"), 2) == 0
         self.quick = {1: even, -1: no(even)}
 
-    def meet(self):
+    def meet(self, meanwhile):
         barrier = pltpu.get_barrier_semaphore()
         sides = [("rows", -1), ("rows", 1), ("cols", -1), ("cols", 1)]
         if self.relays:
@@ -233,6 +233,7 @@
             def _():
                 pl.semaphore_signal(barrier, inc=1, device_id=self.device[side], device_id_type=MESH)
 
+        meanwhile()
         pl.semaphore_wait(barrier, sum(self.here[side].astype(jnp.int32) for side in sides))
 
     def new_recv(self):
@@ -397,7 +398,7 @@
     return rest
 
 
-def step(last, around, grad_ref, padded_ref, out_ref, mid_ref, side_ref, band_ref, relay_ref):
+def step(last, around, grad_ref, padded_ref, out_ref, mid_ref, side_ref, band_ref, relay_ref, meanwhile):
     m = MARGIN
     planes, extent, _ = grad_ref.shape
     wide = extent - 2 * m
@@ -459,28 +460,37 @@
         if not last:
             edges[h, q, d].start()
 
-    def begin_all(quick):
-        for d in (quick, -quick):
-            for q in range(BLOCKS):
-                for h in (-1, 1):
-                    gather(h, q, d)
-                    if q in sent:
-                        bands[h, q, d].start()
+    def in_turn(far, quick):
+        near, straight = [(-far, q, quick) for q in sent], []
+        relayed = [(far, q, quick) for q in sent]
+        for q in sent:
+            straight += [(-far, q, -quick), (far, q, -quick)]
+        return near, straight, relayed
+
+    def begin_all(far, quick):
+        near, straight, relayed = in_turn(far, quick)
+        for h, q, d in near[:1] + relayed + straight + near[1:]:
+            gather(h, q, d)
+            bands[h, q, d].start()
+        for h, q, d in sides:
+            if q not in sent:
+                gather(h, q, d)
 
     def finish_all(far, quick):
-        order = [(-far, q, quick) for q in sent]
-        for q in sent:
-            order += [(far, q, -quick), (-far, q, -quick)]
-        for h, q, d in order + [(far, q, quick) for q in sent]:
+        near, straight, relayed = in_turn(far, quick)
+        for h, q, d in near[:1] + straight + near[1:] + relayed:
             finish(h, BLOCKS - 1 - q, d)
 
-    for quick in (-1, 1):
-        pl.when(around.quick[quick])(functools.partial(begin_all, quick))
+    def by_place(work):
+        for far in (-1, 1):
+            for quick in (-1, 1):
+                pl.when(both(around.far[far], around.quick[quick]))(functools.partial(work, far, quick))
+
+    by_place(begin_all)
     for band in bands.values():
         band.forward()
-    for far in (-1, 1):
-        for quick in (-1, 1):
-            pl.when(both(around.far[far], around.quick[quick]))(functools.partial(finish_all, far, quick))
+    meanwhile()
+    by_place(finish_all)
     for edge in edges.values():
         edge.wait_recv()
     def rest():
@@ -548,10 +558,13 @@
         pltpu.make_async_copy(source, target, local_sems.at[slots * parts + 1 + k])
         for k, (source, target) in enumerate([(probe_from, probe_ref), (table_from, table_ref)])
     ]
-    for copy in [own, *fetches, *held]:
-        copy.start()
     around = Around(send_sems, recv_sems)
-    around.meet()
+
+    def fetch_all():
+        for copy in [*fetches, own, *held]:
+            copy.start()
+
+    around.meet(fetch_all)
 
     def meanwhile():
         grad_ref[...] = jnp.zeros_like(grad_ref)
@@ -571,17 +584,16 @@
             for p in range(planes):
                 probes_ref[slot, p] = roll_probe(live, positions_ref[0, slot], positions_ref[1, slot], probe_ref[p])
 
-    rests = [pad(around, field_ref, padded_refs[0], relay_ref.at[0], meanwhile, afterwards)]
+    rest = pad(around, field_ref, padded_refs[0], relay_ref.at[0], meanwhile, afterwards)
     for k in range(ITERS):
         last = k == ITERS - 1
-        add_terms(
-            positions_ref, padded_refs[k], probes_ref, measured_ref, table_ref, grad_ref.at[k]
-        )
+        add_terms(positions_ref, padded_refs[k], probes_ref, measured_ref, table_ref, grad_ref.at[k])
         target = out_ref if last else padded_refs[k + 1]
         scratch = [ref.at[k] for ref in (mid_ref, side_ref, band_ref)]
-        rests.append(step(last, around, grad_ref.at[k], padded_refs[k], target, *scratch, relay_ref.at[k + 1]))
-    for rest in rests:
-        rest()
+        rest = step(
+            last, around, grad_ref.at[k], padded_refs[k], target, *scratch, relay_ref.at[k + 1], meanwhile=rest
+        )
+    rest()
 
 
 def on_device(object_field, probe, positions, counts, intensity):

time: 71.1 us -> 70 us (0.985); the launches traced: 69.9 us -> 69.9 us
  no operation moved by 1% of the time
where the time goes in v6:
time: 70 us; the launch traced here: 69.9 us
  Pallas kernels  67.7 us (97%)
  local copies, waits for them, and re-layouts  1.47 us (2%)
    pallas_call x1, Pallas kernels, on_device(): pl.pallas_call(whole_kernel, out_shape=jax.ShapeDtypeStruct(object_field....  67.7 us
    unnamed x3, local copies, waits for them, and re-layouts  1.47 us

profile of v6, /device:TPU:5, one launch (start us, length us, event | category | flops | bytes accessed | tf_op | source)
XLA Modules:
  0.0 69.9 jit_solution(522583337515895434)
XLA Ops:
  0.7 0.0 copy-start
  0.7 0.7 copy-done
  1.3 67.7 %whole.1 = f32[2,256,256]{2,1,0:T(8,128)S(1)} custom-call(s32[2,6]{1,0:T(2,128)S(1)} %bitcast.3, s32[1,1]{1,0:T(1,128)S(6)} %copy.8.counts_ref, f32[2,256,256]{2,1,0:T(8,128)} %field_ref.1, s32[1,1,6,256,256]{4,3,2,1,0:T(8,128)} %intensity_ref.1, f32[2,256,256]{2,1,0:T(8,128)} %probe_from.1, bf16[2,4,256,256]{3,2,1,0:T(8,128)(2,1)} %constant.2.clone.table_from), custom_call_target="tpu_custom_call" | custom-call | tf_op jit(solution)/shard_map/whole/pallas_call | solution.py:619
  69.1 0.8 %copy.9 = f32[2,256,256]{2,1,0:T(8,128)} copy(f32[2,256,256]{2,1,0:T(8,128)S(1)} %whole.1) | data formatting | bytes 1048576
Async XLA Ops:
  0.7 0.7 copy-start

commit v7 on v6

--- a/solution.py
+++ b/solution.py
@@ -14,7 +14,7 @@
 LANES = 128
 ROWS = 8
 PAIR = 2
-BLOCKS = 2
+BLOCKS = 4
 
 
 step_rate = 0.02

time: 70 us -> 69.6 us (level)
  no operation moved by 1% of the time
where the time goes in v7:
time: 69.6 us; the launch traced here: 69.5 us
  Pallas kernels  67.3 us (97%)
  local copies, waits for them, and re-layouts  1.47 us (2%)
    pallas_call x1, Pallas kernels, on_device(): pl.pallas_call(whole_kernel, out_shape=jax.ShapeDtypeStruct(object_field....  67.3 us
    unnamed x3, local copies, waits for them, and re-layouts  1.47 us

profile of v7, /device:TPU:5, one launch (start us, length us, event | category | flops | bytes accessed | tf_op | source)
XLA Modules:
  0.0 69.5 jit_solution(10671007731777352837)
XLA Ops:
  0.7 0.0 copy-start
  0.7 0.7 copy-done
  1.3 67.3 %whole.1 = f32[2,256,256]{2,1,0:T(8,128)S(1)} custom-call(s32[2,6]{1,0:T(2,128)S(1)} %bitcast.3, s32[1,1]{1,0:T(1,128)S(6)} %copy.8.counts_ref, f32[2,256,256]{2,1,0:T(8,128)} %field_ref.1, s32[1,1,6,256,256]{4,3,2,1,0:T(8,128)} %intensity_ref.1, f32[2,256,256]{2,1,0:T(8,128)} %probe_from.1, bf16[2,4,256,256]{3,2,1,0:T(8,128)(2,1)} %constant.2.clone.table_from), custom_call_target="tpu_custom_call" | custom-call | tf_op jit(solution)/shard_map/whole/pallas_call | solution.py:619
  68.7 0.8 %copy.9 = f32[2,256,256]{2,1,0:T(8,128)} copy(f32[2,256,256]{2,1,0:T(8,128)S(1)} %whole.1) | data formatting | bytes 1048576
Async XLA Ops:
  0.7 0.7 copy-start
